TPU v7x, 16 devices: a 4x2x1 block of a 4x4x8 slice. The times are simulated.
16 devices in a mesh: dp: 2 (over y, z), cp: 8 (over x, core).
Axes of the slice: x: 4, y: 2, z: 1, core: 2. Of those that a mesh axis runs over, the one named last changes fastest.
The devices are a block of a 4x4x8 slice.
Arguments:
- queries: bfloat16 [768, 32, 128], P(('dp', 'cp')), parts along dimension 0
- key_new: bfloat16 [768, 8, 128], P(('dp', 'cp')), parts along dimension 0
- value_new: bfloat16 [768, 8, 128], P(('dp', 'cp')), parts along dimension 0
- key_cache: bfloat16 [24576, 8, 128], P(('dp', 'cp')), parts along dimension 0
- value_cache: bfloat16 [24576, 8, 128], P(('dp', 'cp')), parts along dimension 0
- prefix_len: int32 [2], P('dp'), parts along dimension 0
Outputs:
- output 1: bfloat16 [768, 32, 128], P(('dp', 'cp')), parts along dimension 0
- output 2: float32 [768, 32], P(('dp', 'cp')), parts along dimension 0
There are 2 independent parts. A program takes and returns all parts, laid end to end along the dimension named above; each array names one.
All inputs are finite; a program needn't handle non-finite values.
Results may differ from a plain program's by a relative error of at most 0.00895518.
Values are sent between devices in bfloat16 or wider.
A program may use at most 768 MiB of HBM per device.

v0:
```python
import jax
import jax.numpy as jnp
from jax import lax
from jax.sharding import PartitionSpec as P

MASK_FILL = -1e30


def solution(mesh):
    groups = mesh.shape['cp']
    send_pairs = [(src_idx, (src_idx + 1) % groups) for src_idx in range(groups)]
    tok_spec = P(('dp', 'cp'))

    def local_attend(queries, key_new, value_new, key_cache, value_cache, prefix_len):
        tok_rows, num_heads, head_dim = queries.shape
        cache_len, kv_heads = key_cache.shape[0], key_cache.shape[1]
        group_ratio = num_heads // kv_heads
        logit_scale = head_dim ** -0.5
        my_rank = lax.axis_index('cp')
        cache_seen = my_rank * cache_len + jnp.arange(cache_len) < prefix_len[0]
        row_ids = jnp.arange(tok_rows)
        key_ids = my_rank * tok_rows + row_ids

        def absorb(loop_step, q_blk, out_acc, row_max, row_sum):
            source = (my_rank - loop_step) % groups
            q_grouped = q_blk.reshape(tok_rows, kv_heads, group_ratio, head_dim)
            s_cache = jnp.einsum('tkgd,skd->kgts', q_grouped, key_cache, preferred_element_type=jnp.float32) * logit_scale
            s_cache = jnp.where(cache_seen, s_cache, MASK_FILL)
            s_fresh = jnp.einsum('tkgd,skd->kgts', q_grouped, key_new, preferred_element_type=jnp.float32) * logit_scale
            fresh_seen = key_ids[None, :] <= (source * tok_rows + row_ids)[:, None]
            s_fresh = jnp.where(fresh_seen, s_fresh, MASK_FILL)
            next_max = jnp.maximum(row_max, jnp.maximum(s_cache.max(axis=-1), s_fresh.max(axis=-1)))
            e_cache = jnp.exp(s_cache - next_max[..., None])
            e_fresh = jnp.exp(s_fresh - next_max[..., None])
            rescale_by = jnp.exp(row_max - next_max)
            row_sum = row_sum * rescale_by + e_cache.sum(axis=-1) + e_fresh.sum(axis=-1)
            out_acc = (out_acc * rescale_by[..., None]
                       + jnp.einsum('kgts,skd->kgtd', e_cache.astype(jnp.bfloat16), value_cache, preferred_element_type=jnp.float32)
                       + jnp.einsum('kgts,skd->kgtd', e_fresh.astype(jnp.bfloat16), value_new, preferred_element_type=jnp.float32))
            return out_acc, next_max, row_sum

        def one_step(loop_step, state):
            q_blk, out_acc, row_max, row_sum = state
            out_acc, row_max, row_sum = absorb(loop_step, q_blk, out_acc, row_max, row_sum)
            return lax.ppermute((q_blk, out_acc, row_max, row_sum), 'cp', send_pairs)

        start_acc = jnp.zeros((kv_heads, group_ratio, tok_rows, head_dim), jnp.float32)
        start_max = jnp.full((kv_heads, group_ratio, tok_rows), MASK_FILL, jnp.float32)
        start_sum = jnp.zeros((kv_heads, group_ratio, tok_rows), jnp.float32)
        q_blk, out_acc, row_max, row_sum = lax.fori_loop(0, groups - 1, one_step, (queries, start_acc, start_max, start_sum))
        out_acc, row_max, row_sum = absorb(groups - 1, q_blk, out_acc, row_max, row_sum)
        out_acc, row_max, row_sum = lax.ppermute((out_acc, row_max, row_sum), 'cp', send_pairs)
        attn_out = (out_acc / row_sum[..., None]).transpose(2, 0, 1, 3).reshape(tok_rows, num_heads, head_dim).astype(jnp.bfloat16)
        row_lse = (row_max + jnp.log(row_sum)).transpose(2, 0, 1).reshape(tok_rows, num_heads)
        return attn_out, row_lse

    return jax.shard_map(local_attend, mesh=mesh, in_specs=(tok_spec, tok_spec, tok_spec, tok_spec, tok_spec, P('dp')), out_specs=(tok_spec, tok_spec), check_vma=False)
```

profile of v0, /device:TPU:112, one launch (start us, length us, event | category | flops | bytes accessed | tf_op | source)
XLA Modules:
  0.0 255.9 jit_solution(5558905221867329424)
XLA Ops:
  1.3 1.9 copy.9
  3.2 2.3 copy.10
  7.1 4.0 %copy.12 = bf16[1536,8,128]{2,0,1:T(8,128)(2,1)} copy(bf16[1536,8,128]{2,1,0:T(8,128)(2,1)} %param.12) | data formatting | bytes 6291456
  15.1 212.2 %while.22 = (s32[]{:T(128)}, bf16[48,32,128]{2,0,1:T(8,128)(2,1)}, f32[8,4,48,128]{3,2,1,0:T(8,128)}, f32[8,4,48]{2,1,0:T(4,128)}, f32[8,4,48]{2,1,0:T(4,128)}, ...) while((s32[]{:T(128)}, bf16[48,32,128]{2,0,1:T(8,128)(2,1)}, ...), condition=%wide.region_5.6_spmd.clone, body=%wide.region_0.5_spmd.clone.sunk | while | flops 1272775040 | bytes 58674984 | solution.py:50
  20.0 2.1 fusion.84
  23.5 3.5 %fusion.85 = f32[8,4,48,128]{3,2,1,0:T(8,128)S(1)} fusion(bf16[1536,8,128]{2,0,1:T(8,128)(2,1)S(1)} %copy-done.3, f32[8,1536,48,4]{1,2,3,0:T(8,128)S(1)} %get-tuple-element.497, f32[8,4,48]{2,1,0:T(4,128)S(1)} %bitcast.146, pred[1536]{0:T(1024)(128)(4,1)S(1)} %add_compare_fusion.3, f32[8,4,48,128]{3,2,1,0:T(8,128)} %get-tuple-element.523, ...), kind=kOutput, calls=%fused_computation.21.clone.1 | convolution fusion | flops 613810176 | bytes 14169600 | tf_op jit(solution)/shard_map/while/body/eval_jaxpr/kgts,skd->kgtd/dot_general | solution.py:38
  28.2 2.5 collective-permute-start
  30.7 1.7 collective-permute-start.3
  32.4 13.2 %collective-permute-done.2 = f32[8,4,48]{2,1,0:T(4,128)} collective-permute-done((f32[8,4,48]{2,1,0:T(4,128)S(1)}, f32[8,4,48]{2,1,0:T(4,128)}, u32[]{:S(2)}, u32[]{:S(2)}) %collective-permute-start.2) | collective-permute-done | bytes 6176 | tf_op jit(solution)/shard_map/while/body/eval_jaxpr/ppermute | solution.py:45
  50.7 2.1 fusion.84
  54.2 3.5 %fusion.85 = f32[8,4,48,128]{3,2,1,0:T(8,128)S(1)} fusion(bf16[1536,8,128]{2,0,1:T(8,128)(2,1)S(1)} %copy-done.3, f32[8,1536,48,4]{1,2,3,0:T(8,128)S(1)} %get-tuple-element.497, f32[8,4,48]{2,1,0:T(4,128)S(1)} %bitcast.146, pred[1536]{0:T(1024)(128)(4,1)S(1)} %add_compare_fusion.3, f32[8,4,48,128]{3,2,1,0:T(8,128)} %get-tuple-element.523, ...), kind=kOutput, calls=%fused_computation.21.clone.1 | convolution fusion | flops 613810176 | bytes 14169600 | tf_op jit(solution)/shard_map/while/body/eval_jaxpr/kgts,skd->kgtd/dot_general | solution.py:38
  59.7 1.7 collective-permute-start.3
  61.4 14.5 %collective-permute-done.2 = f32[8,4,48]{2,1,0:T(4,128)} collective-permute-done((f32[8,4,48]{2,1,0:T(4,128)S(1)}, f32[8,4,48]{2,1,0:T(4,128)}, u32[]{:S(2)}, u32[]{:S(2)}) %collective-permute-start.2) | collective-permute-done | bytes 6176 | tf_op jit(solution)/shard_map/while/body/eval_jaxpr/ppermute | solution.py:45
  80.9 2.1 fusion.84
  84.4 3.5 %fusion.85 = f32[8,4,48,128]{3,2,1,0:T(8,128)S(1)} fusion(bf16[1536,8,128]{2,0,1:T(8,128)(2,1)S(1)} %copy-done.3, f32[8,1536,48,4]{1,2,3,0:T(8,128)S(1)} %get-tuple-element.497, f32[8,4,48]{2,1,0:T(4,128)S(1)} %bitcast.146, pred[1536]{0:T(1024)(128)(4,1)S(1)} %add_compare_fusion.3, f32[8,4,48,128]{3,2,1,0:T(8,128)} %get-tuple-element.523, ...), kind=kOutput, calls=%fused_computation.21.clone.1 | convolution fusion | flops 613810176 | bytes 14169600 | tf_op jit(solution)/shard_map/while/body/eval_jaxpr/kgts,skd->kgtd/dot_general | solution.py:38
  90.5 15.7 %collective-permute-done.2 = f32[8,4,48]{2,1,0:T(4,128)} collective-permute-done((f32[8,4,48]{2,1,0:T(4,128)S(1)}, f32[8,4,48]{2,1,0:T(4,128)}, u32[]{:S(2)}, u32[]{:S(2)}) %collective-permute-start.2) | collective-permute-done | bytes 6176 | tf_op jit(solution)/shard_map/while/body/eval_jaxpr/ppermute | solution.py:45
  111.2 2.1 fusion.84
  114.7 3.5 %fusion.85 = f32[8,4,48,128]{3,2,1,0:T(8,128)S(1)} fusion(bf16[1536,8,128]{2,0,1:T(8,128)(2,1)S(1)} %copy-done.3, f32[8,1536,48,4]{1,2,3,0:T(8,128)S(1)} %get-tuple-element.497, f32[8,4,48]{2,1,0:T(4,128)S(1)} %bitcast.146, pred[1536]{0:T(1024)(128)(4,1)S(1)} %add_compare_fusion.3, f32[8,4,48,128]{3,2,1,0:T(8,128)} %get-tuple-element.523, ...), kind=kOutput, calls=%fused_computation.21.clone.1 | convolution fusion | flops 613810176 | bytes 14169600 | tf_op jit(solution)/shard_map/while/body/eval_jaxpr/kgts,skd->kgtd/dot_general | solution.py:38
  119.5 16.9 %collective-permute-done.2 = f32[8,4,48]{2,1,0:T(4,128)} collective-permute-done((f32[8,4,48]{2,1,0:T(4,128)S(1)}, f32[8,4,48]{2,1,0:T(4,128)}, u32[]{:S(2)}, u32[]{:S(2)}) %collective-permute-start.2) | collective-permute-done | bytes 6176 | tf_op jit(solution)/shard_map/while/body/eval_jaxpr/ppermute | solution.py:45
  141.4 2.1 fusion.84
  144.9 3.5 %fusion.85 = f32[8,4,48,128]{3,2,1,0:T(8,128)S(1)} fusion(bf16[1536,8,128]{2,0,1:T(8,128)(2,1)S(1)} %copy-done.3, f32[8,1536,48,4]{1,2,3,0:T(8,128)S(1)} %get-tuple-element.497, f32[8,4,48]{2,1,0:T(4,128)S(1)} %bitcast.146, pred[1536]{0:T(1024)(128)(4,1)S(1)} %add_compare_fusion.3, f32[8,4,48,128]{3,2,1,0:T(8,128)} %get-tuple-element.523, ...), kind=kOutput, calls=%fused_computation.21.clone.1 | convolution fusion | flops 613810176 | bytes 14169600 | tf_op jit(solution)/shard_map/while/body/eval_jaxpr/kgts,skd->kgtd/dot_general | solution.py:38
  149.7 16.9 %collective-permute-done.2 = f32[8,4,48]{2,1,0:T(4,128)} collective-permute-done((f32[8,4,48]{2,1,0:T(4,128)S(1)}, f32[8,4,48]{2,1,0:T(4,128)}, u32[]{:S(2)}, u32[]{:S(2)}) %collective-permute-start.2) | collective-permute-done | bytes 6176 | tf_op jit(solution)/shard_map/while/body/eval_jaxpr/ppermute | solution.py:45
  171.6 2.1 fusion.84
  175.2 3.5 %fusion.85 = f32[8,4,48,128]{3,2,1,0:T(8,128)S(1)} fusion(bf16[1536,8,128]{2,0,1:T(8,128)(2,1)S(1)} %copy-done.3, f32[8,1536,48,4]{1,2,3,0:T(8,128)S(1)} %get-tuple-element.497, f32[8,4,48]{2,1,0:T(4,128)S(1)} %bitcast.146, pred[1536]{0:T(1024)(128)(4,1)S(1)} %add_compare_fusion.3, f32[8,4,48,128]{3,2,1,0:T(8,128)} %get-tuple-element.523, ...), kind=kOutput, calls=%fused_computation.21.clone.1 | convolution fusion | flops 613810176 | bytes 14169600 | tf_op jit(solution)/shard_map/while/body/eval_jaxpr/kgts,skd->kgtd/dot_general | solution.py:38
  180.0 16.9 %collective-permute-done.2 = f32[8,4,48]{2,1,0:T(4,128)} collective-permute-done((f32[8,4,48]{2,1,0:T(4,128)S(1)}, f32[8,4,48]{2,1,0:T(4,128)}, u32[]{:S(2)}, u32[]{:S(2)}) %collective-permute-start.2) | collective-permute-done | bytes 6176 | tf_op jit(solution)/shard_map/while/body/eval_jaxpr/ppermute | solution.py:45
  201.9 2.1 fusion.84
  205.4 3.5 %fusion.85 = f32[8,4,48,128]{3,2,1,0:T(8,128)S(1)} fusion(bf16[1536,8,128]{2,0,1:T(8,128)(2,1)S(1)} %copy-done.3, f32[8,1536,48,4]{1,2,3,0:T(8,128)S(1)} %get-tuple-element.497, f32[8,4,48]{2,1,0:T(4,128)S(1)} %bitcast.146, pred[1536]{0:T(1024)(128)(4,1)S(1)} %add_compare_fusion.3, f32[8,4,48,128]{3,2,1,0:T(8,128)} %get-tuple-element.523, ...), kind=kOutput, calls=%fused_computation.21.clone.1 | convolution fusion | flops 613810176 | bytes 14169600 | tf_op jit(solution)/shard_map/while/body/eval_jaxpr/kgts,skd->kgtd/dot_general | solution.py:38
  210.2 16.9 %collective-permute-done.2 = f32[8,4,48]{2,1,0:T(4,128)} collective-permute-done((f32[8,4,48]{2,1,0:T(4,128)S(1)}, f32[8,4,48]{2,1,0:T(4,128)}, u32[]{:S(2)}, u32[]{:S(2)}) %collective-permute-start.2) | collective-permute-done | bytes 6176 | tf_op jit(solution)/shard_map/while/body/eval_jaxpr/ppermute | solution.py:45
  227.3 3.8 %bitcast_reduce_fusion.1 = (f32[8,4,48]{2,1,0:T(4,128)S(1)}, f32[8,48,4,1536]{3,1,2,0:T(8,128)S(1)}) fusion(pred[1536]{0:T(1024)(128)(4,1)} %add_compare_fusion.1, bf16[48,8,4,128]{3,0,2,1:T(8,128)(2,1)} %bitcast.1, bf16[1536,8,128,1]{2,1,0,3:T(8,128)(2,1)} %bitcast.143), kind=kOutput, calls=%fused_computation.38 | convolution fusion | flops 611056128 | bytes 12983808 | tf_op jit(solution)/shard_map/tkgd,skd->kgts/dot_general | solution.py:27
  233.8 2.1 fusion.34
  236.7 4.0 %fusion.47 = f32[8,4,48,128]{3,2,1,0:T(8,128)S(1)} fusion(bf16[1536,8,128,1]{2,1,0,3:T(8,128)(2,1)S(1)} %bitcast.149, f32[8,48,4,1536]{3,1,2,0:T(8,128)S(1)} %get-tuple-element.401, f32[8,4,48]{2,1,0:T(4,128)S(1)} %bitcast.157, pred[1536]{0:T(1024)(128)(4,1)S(1)} %copy-done.7, f32[8,4,48,128]{3,2,1,0:T(8,128)} %get-tuple-element.314, ...), kind=kOutput, calls=%fused_computation.55 | convolution fusion | flops 613810176 | bytes 14169600 | tf_op jit(solution)/shard_map/kgts,skd->kgtd/dot_general | solution.py:38
  241.3 12.6 %collective-permute-done.5 = f32[8,4,48]{2,1,0:T(4,128)S(1)} collective-permute-done((f32[8,4,48]{2,1,0:T(4,128)S(1)}, f32[8,4,48]{2,1,0:T(4,128)S(1)}, u32[]{:S(2)}, u32[]{:S(2)}) %collective-permute-start.5) | collective-permute-done | bytes 6176 | tf_op jit(solution)/shard_map/ppermute | solution.py:52
  (198 shorter events, 67.3 us)
Async XLA Ops:
  0.6 10.4 %copy-start.4 = (bf16[48,8,128]{2,1,0:T(8,128)(2,1)S(1)}, bf16[48,8,128]{2,1,0:T(8,128)(2,1)}, u32[]{:S(2)}) copy-start(bf16[48,8,128]{2,1,0:T(8,128)(2,1)} %param.10) | copy-start | bytes 294916
  28.2 17.6 %collective-permute-start.1 = (f32[8,4,48,128]{3,2,1,0:T(8,128)}, f32[8,4,48,128]{3,2,1,0:T(8,128)}, u32[]{:S(2)}, u32[]{:S(2)}) collective-permute-start(f32[8,4,48,128]{3,2,1,0:T(8,128)} %convolution_add_fusion.3), channel_id=1, source_target_pairs={{0,1},{1,2},{2,3},{3,4},{4,5},{5,6},{6,7},{7,0},{8,9},{9,10},{10,1... | collective-permute-start | bytes 2359304 | tf_op jit(solution)/shard_map/while/body/eval_jaxpr/ppermute | solution.py:45
  28.2 17.6 %collective-permute-start = (bf16[48,32,128]{2,0,1:T(8,128)(2,1)S(1)}, bf16[48,32,128]{2,0,1:T(8,128)(2,1)}, u32[]{:S(2)}, u32[]{:S(2)}) collective-permute-start(bf16[48,32,128]{2,0,1:T(8,128)(2,1)S(1)} %copy.58), channel_id=1, source_target_pairs={{0,1},{1,2},{2,3},{3,4},{4,5},{5,6},{6,7},{7,0},{8,9},{9,10},{10,1... | collective-permute-start | bytes 1179656 | tf_op jit(solution)/shard_map/while/body/eval_jaxpr/ppermute | solution.py:45
  30.6 15.0 %collective-permute-start.2 = (f32[8,4,48]{2,1,0:T(4,128)S(1)}, f32[8,4,48]{2,1,0:T(4,128)}, u32[]{:S(2)}, u32[]{:S(2)}) collective-permute-start(f32[8,4,48]{2,1,0:T(4,128)S(1)} %bitcast.148), channel_id=1, source_target_pairs={{0,1},{1,2},{2,3},{3,4},{4,5},{5,6},{6,7},{7,0},{8,9},{9,10},{10,1... | collective-permute-start | bytes 18440 | tf_op jit(solution)/shard_map/while/body/eval_jaxpr/ppermute | solution.py:45
  30.7 15.1 %collective-permute-start.3 = (f32[8,4,48]{2,1,0:T(4,128)}, f32[8,4,48]{2,1,0:T(4,128)}, u32[]{:S(2)}, u32[]{:S(2)}) collective-permute-start(f32[8,4,48]{2,1,0:T(4,128)} %bitcast.138), channel_id=1, source_target_pairs={{0,1},{1,2},{2,3},{3,4},{4,5},{5,6},{6,7},{7,0},{8,9},{9,10},{10,1... | collective-permute-start | bytes 18440 | tf_op jit(solution)/shard_map/while/body/eval_jaxpr/ppermute | solution.py:45
  58.9 17.2 %collective-permute-start.1 = (f32[8,4,48,128]{3,2,1,0:T(8,128)}, f32[8,4,48,128]{3,2,1,0:T(8,128)}, u32[]{:S(2)}, u32[]{:S(2)}) collective-permute-start(f32[8,4,48,128]{3,2,1,0:T(8,128)} %convolution_add_fusion.3), channel_id=1, source_target_pairs={{0,1},{1,2},{2,3},{3,4},{4,5},{5,6},{6,7},{7,0},{8,9},{9,10},{10,1... | collective-permute-start | bytes 2359304 | tf_op jit(solution)/shard_map/while/body/eval_jaxpr/ppermute | solution.py:45
  58.9 17.2 %collective-permute-start = (bf16[48,32,128]{2,0,1:T(8,128)(2,1)S(1)}, bf16[48,32,128]{2,0,1:T(8,128)(2,1)}, u32[]{:S(2)}, u32[]{:S(2)}) collective-permute-start(bf16[48,32,128]{2,0,1:T(8,128)(2,1)S(1)} %copy.58), channel_id=1, source_target_pairs={{0,1},{1,2},{2,3},{3,4},{4,5},{5,6},{6,7},{7,0},{8,9},{9,10},{10,1... | collective-permute-start | bytes 1179656 | tf_op jit(solution)/shard_map/while/body/eval_jaxpr/ppermute | solution.py:45
  59.7 16.2 %collective-permute-start.2 = (f32[8,4,48]{2,1,0:T(4,128)S(1)}, f32[8,4,48]{2,1,0:T(4,128)}, u32[]{:S(2)}, u32[]{:S(2)}) collective-permute-start(f32[8,4,48]{2,1,0:T(4,128)S(1)} %bitcast.148), channel_id=1, source_target_pairs={{0,1},{1,2},{2,3},{3,4},{4,5},{5,6},{6,7},{7,0},{8,9},{9,10},{10,1... | collective-permute-start | bytes 18440 | tf_op jit(solution)/shard_map/while/body/eval_jaxpr/ppermute | solution.py:45
  59.7 16.4 %collective-permute-start.3 = (f32[8,4,48]{2,1,0:T(4,128)}, f32[8,4,48]{2,1,0:T(4,128)}, u32[]{:S(2)}, u32[]{:S(2)}) collective-permute-start(f32[8,4,48]{2,1,0:T(4,128)} %bitcast.138), channel_id=1, source_target_pairs={{0,1},{1,2},{2,3},{3,4},{4,5},{5,6},{6,7},{7,0},{8,9},{9,10},{10,1... | collective-permute-start | bytes 18440 | tf_op jit(solution)/shard_map/while/body/eval_jaxpr/ppermute | solution.py:45
  89.1 17.2 %collective-permute-start.1 = (f32[8,4,48,128]{3,2,1,0:T(8,128)}, f32[8,4,48,128]{3,2,1,0:T(8,128)}, u32[]{:S(2)}, u32[]{:S(2)}) collective-permute-start(f32[8,4,48,128]{3,2,1,0:T(8,128)} %convolution_add_fusion.3), channel_id=1, source_target_pairs={{0,1},{1,2},{2,3},{3,4},{4,5},{5,6},{6,7},{7,0},{8,9},{9,10},{10,1... | collective-permute-start | bytes 2359304 | tf_op jit(solution)/shard_map/while/body/eval_jaxpr/ppermute | solution.py:45
  89.1 17.2 %collective-permute-start = (bf16[48,32,128]{2,0,1:T(8,128)(2,1)S(1)}, bf16[48,32,128]{2,0,1:T(8,128)(2,1)}, u32[]{:S(2)}, u32[]{:S(2)}) collective-permute-start(bf16[48,32,128]{2,0,1:T(8,128)(2,1)S(1)} %copy.58), channel_id=1, source_target_pairs={{0,1},{1,2},{2,3},{3,4},{4,5},{5,6},{6,7},{7,0},{8,9},{9,10},{10,1... | collective-permute-start | bytes 1179656 | tf_op jit(solution)/shard_map/while/body/eval_jaxpr/ppermute | solution.py:45
  89.1 17.0 %collective-permute-start.2 = (f32[8,4,48]{2,1,0:T(4,128)S(1)}, f32[8,4,48]{2,1,0:T(4,128)}, u32[]{:S(2)}, u32[]{:S(2)}) collective-permute-start(f32[8,4,48]{2,1,0:T(4,128)S(1)} %bitcast.148), channel_id=1, source_target_pairs={{0,1},{1,2},{2,3},{3,4},{4,5},{5,6},{6,7},{7,0},{8,9},{9,10},{10,1... | collective-permute-start | bytes 18440 | tf_op jit(solution)/shard_map/while/body/eval_jaxpr/ppermute | solution.py:45
  89.1 17.2 %collective-permute-start.3 = (f32[8,4,48]{2,1,0:T(4,128)}, f32[8,4,48]{2,1,0:T(4,128)}, u32[]{:S(2)}, u32[]{:S(2)}) collective-permute-start(f32[8,4,48]{2,1,0:T(4,128)} %bitcast.138), channel_id=1, source_target_pairs={{0,1},{1,2},{2,3},{3,4},{4,5},{5,6},{6,7},{7,0},{8,9},{9,10},{10,1... | collective-permute-start | bytes 18440 | tf_op jit(solution)/shard_map/while/body/eval_jaxpr/ppermute | solution.py:45
  119.4 17.2 %collective-permute-start.1 = (f32[8,4,48,128]{3,2,1,0:T(8,128)}, f32[8,4,48,128]{3,2,1,0:T(8,128)}, u32[]{:S(2)}, u32[]{:S(2)}) collective-permute-start(f32[8,4,48,128]{3,2,1,0:T(8,128)} %convolution_add_fusion.3), channel_id=1, source_target_pairs={{0,1},{1,2},{2,3},{3,4},{4,5},{5,6},{6,7},{7,0},{8,9},{9,10},{10,1... | collective-permute-start | bytes 2359304 | tf_op jit(solution)/shard_map/while/body/eval_jaxpr/ppermute | solution.py:45
  119.4 17.2 %collective-permute-start = (bf16[48,32,128]{2,0,1:T(8,128)(2,1)S(1)}, bf16[48,32,128]{2,0,1:T(8,128)(2,1)}, u32[]{:S(2)}, u32[]{:S(2)}) collective-permute-start(bf16[48,32,128]{2,0,1:T(8,128)(2,1)S(1)} %copy.58), channel_id=1, source_target_pairs={{0,1},{1,2},{2,3},{3,4},{4,5},{5,6},{6,7},{7,0},{8,9},{9,10},{10,1... | collective-permute-start | bytes 1179656 | tf_op jit(solution)/shard_map/while/body/eval_jaxpr/ppermute | solution.py:45
  119.4 17.0 %collective-permute-start.2 = (f32[8,4,48]{2,1,0:T(4,128)S(1)}, f32[8,4,48]{2,1,0:T(4,128)}, u32[]{:S(2)}, u32[]{:S(2)}) collective-permute-start(f32[8,4,48]{2,1,0:T(4,128)S(1)} %bitcast.148), channel_id=1, source_target_pairs={{0,1},{1,2},{2,3},{3,4},{4,5},{5,6},{6,7},{7,0},{8,9},{9,10},{10,1... | collective-permute-start | bytes 18440 | tf_op jit(solution)/shard_map/while/body/eval_jaxpr/ppermute | solution.py:45
  119.4 17.2 %collective-permute-start.3 = (f32[8,4,48]{2,1,0:T(4,128)}, f32[8,4,48]{2,1,0:T(4,128)}, u32[]{:S(2)}, u32[]{:S(2)}) collective-permute-start(f32[8,4,48]{2,1,0:T(4,128)} %bitcast.138), channel_id=1, source_target_pairs={{0,1},{1,2},{2,3},{3,4},{4,5},{5,6},{6,7},{7,0},{8,9},{9,10},{10,1... | collective-permute-start | bytes 18440 | tf_op jit(solution)/shard_map/while/body/eval_jaxpr/ppermute | solution.py:45
  149.6 17.2 %collective-permute-start.1 = (f32[8,4,48,128]{3,2,1,0:T(8,128)}, f32[8,4,48,128]{3,2,1,0:T(8,128)}, u32[]{:S(2)}, u32[]{:S(2)}) collective-permute-start(f32[8,4,48,128]{3,2,1,0:T(8,128)} %convolution_add_fusion.3), channel_id=1, source_target_pairs={{0,1},{1,2},{2,3},{3,4},{4,5},{5,6},{6,7},{7,0},{8,9},{9,10},{10,1... | collective-permute-start | bytes 2359304 | tf_op jit(solution)/shard_map/while/body/eval_jaxpr/ppermute | solution.py:45
  149.6 17.2 %collective-permute-start = (bf16[48,32,128]{2,0,1:T(8,128)(2,1)S(1)}, bf16[48,32,128]{2,0,1:T(8,128)(2,1)}, u32[]{:S(2)}, u32[]{:S(2)}) collective-permute-start(bf16[48,32,128]{2,0,1:T(8,128)(2,1)S(1)} %copy.58), channel_id=1, source_target_pairs={{0,1},{1,2},{2,3},{3,4},{4,5},{5,6},{6,7},{7,0},{8,9},{9,10},{10,1... | collective-permute-start | bytes 1179656 | tf_op jit(solution)/shard_map/while/body/eval_jaxpr/ppermute | solution.py:45
  149.6 17.0 %collective-permute-start.2 = (f32[8,4,48]{2,1,0:T(4,128)S(1)}, f32[8,4,48]{2,1,0:T(4,128)}, u32[]{:S(2)}, u32[]{:S(2)}) collective-permute-start(f32[8,4,48]{2,1,0:T(4,128)S(1)} %bitcast.148), channel_id=1, source_target_pairs={{0,1},{1,2},{2,3},{3,4},{4,5},{5,6},{6,7},{7,0},{8,9},{9,10},{10,1... | collective-permute-start | bytes 18440 | tf_op jit(solution)/shard_map/while/body/eval_jaxpr/ppermute | solution.py:45
  149.6 17.2 %collective-permute-start.3 = (f32[8,4,48]{2,1,0:T(4,128)}, f32[8,4,48]{2,1,0:T(4,128)}, u32[]{:S(2)}, u32[]{:S(2)}) collective-permute-start(f32[8,4,48]{2,1,0:T(4,128)} %bitcast.138), channel_id=1, source_target_pairs={{0,1},{1,2},{2,3},{3,4},{4,5},{5,6},{6,7},{7,0},{8,9},{9,10},{10,1... | collective-permute-start | bytes 18440 | tf_op jit(solution)/shard_map/while/body/eval_jaxpr/ppermute | solution.py:45
  179.9 17.2 %collective-permute-start.1 = (f32[8,4,48,128]{3,2,1,0:T(8,128)}, f32[8,4,48,128]{3,2,1,0:T(8,128)}, u32[]{:S(2)}, u32[]{:S(2)}) collective-permute-start(f32[8,4,48,128]{3,2,1,0:T(8,128)} %convolution_add_fusion.3), channel_id=1, source_target_pairs={{0,1},{1,2},{2,3},{3,4},{4,5},{5,6},{6,7},{7,0},{8,9},{9,10},{10,1... | collective-permute-start | bytes 2359304 | tf_op jit(solution)/shard_map/while/body/eval_jaxpr/ppermute | solution.py:45
  179.9 17.2 %collective-permute-start = (bf16[48,32,128]{2,0,1:T(8,128)(2,1)S(1)}, bf16[48,32,128]{2,0,1:T(8,128)(2,1)}, u32[]{:S(2)}, u32[]{:S(2)}) collective-permute-start(bf16[48,32,128]{2,0,1:T(8,128)(2,1)S(1)} %copy.58), channel_id=1, source_target_pairs={{0,1},{1,2},{2,3},{3,4},{4,5},{5,6},{6,7},{7,0},{8,9},{9,10},{10,1... | collective-permute-start | bytes 1179656 | tf_op jit(solution)/shard_map/while/body/eval_jaxpr/ppermute | solution.py:45
  179.9 17.0 %collective-permute-start.2 = (f32[8,4,48]{2,1,0:T(4,128)S(1)}, f32[8,4,48]{2,1,0:T(4,128)}, u32[]{:S(2)}, u32[]{:S(2)}) collective-permute-start(f32[8,4,48]{2,1,0:T(4,128)S(1)} %bitcast.148), channel_id=1, source_target_pairs={{0,1},{1,2},{2,3},{3,4},{4,5},{5,6},{6,7},{7,0},{8,9},{9,10},{10,1... | collective-permute-start | bytes 18440 | tf_op jit(solution)/shard_map/while/body/eval_jaxpr/ppermute | solution.py:45
  179.9 17.2 %collective-permute-start.3 = (f32[8,4,48]{2,1,0:T(4,128)}, f32[8,4,48]{2,1,0:T(4,128)}, u32[]{:S(2)}, u32[]{:S(2)}) collective-permute-start(f32[8,4,48]{2,1,0:T(4,128)} %bitcast.138), channel_id=1, source_target_pairs={{0,1},{1,2},{2,3},{3,4},{4,5},{5,6},{6,7},{7,0},{8,9},{9,10},{10,1... | collective-permute-start | bytes 18440 | tf_op jit(solution)/shard_map/while/body/eval_jaxpr/ppermute | solution.py:45
  210.1 17.2 %collective-permute-start.1 = (f32[8,4,48,128]{3,2,1,0:T(8,128)}, f32[8,4,48,128]{3,2,1,0:T(8,128)}, u32[]{:S(2)}, u32[]{:S(2)}) collective-permute-start(f32[8,4,48,128]{3,2,1,0:T(8,128)} %convolution_add_fusion.3), channel_id=1, source_target_pairs={{0,1},{1,2},{2,3},{3,4},{4,5},{5,6},{6,7},{7,0},{8,9},{9,10},{10,1... | collective-permute-start | bytes 2359304 | tf_op jit(solution)/shard_map/while/body/eval_jaxpr/ppermute | solution.py:45
  210.1 17.2 %collective-permute-start = (bf16[48,32,128]{2,0,1:T(8,128)(2,1)S(1)}, bf16[48,32,128]{2,0,1:T(8,128)(2,1)}, u32[]{:S(2)}, u32[]{:S(2)}) collective-permute-start(bf16[48,32,128]{2,0,1:T(8,128)(2,1)S(1)} %copy.58), channel_id=1, source_target_pairs={{0,1},{1,2},{2,3},{3,4},{4,5},{5,6},{6,7},{7,0},{8,9},{9,10},{10,1... | collective-permute-start | bytes 1179656 | tf_op jit(solution)/shard_map/while/body/eval_jaxpr/ppermute | solution.py:45
  210.1 17.0 %collective-permute-start.2 = (f32[8,4,48]{2,1,0:T(4,128)S(1)}, f32[8,4,48]{2,1,0:T(4,128)}, u32[]{:S(2)}, u32[]{:S(2)}) collective-permute-start(f32[8,4,48]{2,1,0:T(4,128)S(1)} %bitcast.148), channel_id=1, source_target_pairs={{0,1},{1,2},{2,3},{3,4},{4,5},{5,6},{6,7},{7,0},{8,9},{9,10},{10,1... | collective-permute-start | bytes 18440 | tf_op jit(solution)/shard_map/while/body/eval_jaxpr/ppermute | solution.py:45
  210.1 17.2 %collective-permute-start.3 = (f32[8,4,48]{2,1,0:T(4,128)}, f32[8,4,48]{2,1,0:T(4,128)}, u32[]{:S(2)}, u32[]{:S(2)}) collective-permute-start(f32[8,4,48]{2,1,0:T(4,128)} %bitcast.138), channel_id=1, source_target_pairs={{0,1},{1,2},{2,3},{3,4},{4,5},{5,6},{6,7},{7,0},{8,9},{9,10},{10,1... | collective-permute-start | bytes 18440 | tf_op jit(solution)/shard_map/while/body/eval_jaxpr/ppermute | solution.py:45
  241.1 13.6 %collective-permute-start.4 = (f32[8,4,48,128]{3,2,1,0:T(8,128)S(1)}, f32[8,4,48,128]{3,2,1,0:T(8,128)S(1)}, u32[]{:S(2)}, u32[]{:S(2)}) collective-permute-start(f32[8,4,48,128]{3,2,1,0:T(8,128)S(1)} %convolution_add_fusion.1), channel_id=1, source_target_pairs={{0,1},{1,2},{2,3},{3,4},{4,5},{5,6},{6,7},{7,0},{8,9},{9,10},{10,1... | collective-permute-start | bytes 2359304 | tf_op jit(solution)/shard_map/ppermute | solution.py:52
  241.2 12.8 %collective-permute-start.5 = (f32[8,4,48]{2,1,0:T(4,128)S(1)}, f32[8,4,48]{2,1,0:T(4,128)S(1)}, u32[]{:S(2)}, u32[]{:S(2)}) collective-permute-start(f32[8,4,48]{2,1,0:T(4,128)S(1)} %bitcast.168), channel_id=1, source_target_pairs={{0,1},{1,2},{2,3},{3,4},{4,5},{5,6},{6,7},{7,0},{8,9},{9,10},{10,1... | collective-permute-start | bytes 18440 | tf_op jit(solution)/shard_map/ppermute | solution.py:52
  241.2 12.9 %collective-permute-start.6 = (f32[8,4,48]{2,1,0:T(4,128)S(1)}, f32[8,4,48]{2,1,0:T(4,128)S(1)}, u32[]{:S(2)}, u32[]{:S(2)}) collective-permute-start(f32[8,4,48]{2,1,0:T(4,128)S(1)} %bitcast.159), channel_id=1, source_target_pairs={{0,1},{1,2},{2,3},{3,4},{4,5},{5,6},{6,7},{7,0},{8,9},{9,10},{10,1... | collective-permute-start | bytes 18440 | tf_op jit(solution)/shard_map/ppermute | solution.py:52
  (26 other events, 120.4 us)
where the time goes:
time: 257 us; the launch traced here: 256 us
  waiting for transfers between devices  125 us (49%)
  matrix products  57.6 us (22%)
  other arithmetic  42.2 us (16%)
  local copies, waits for them, and re-layouts  20.5 us (8%)
  starting transfers between devices  8.68 us (3%)
    ppermute x28, waiting for transfers between devices, one_step(): return lax.ppermute((q_blk, out_acc, row_max, row_sum), 'cp', send_pairs)  112 us
    dot_general x8, matrix products, absorb(): jnp.einsum('kgts,skd->kgtd', e_cache.astype(jnp.bfloat16), value_cache, p...  28.3 us
    reduce_sum x16, other arithmetic, absorb(): row_sum = row_sum * rescale_by + e_cache.sum(axis=-1) + e_fresh.sum(axis=-1)  18.4 us
    dot_general x8, matrix products, absorb(): jnp.einsum('tkgd,skd->kgts', q_grouped, key_cache, preferred_element_type...  14.7 us
    ppermute x3, waiting for transfers between devices, local_attend(): lax.ppermute((out_acc, row_max, row_sum), 'cp', send_pairs)  12.8 us
    unnamed x18, local copies, waits for them, and re-layouts  11.2 us
    add x8, other arithmetic, absorb(): row_sum = row_sum * rescale_by + e_cache.sum(axis=-1) + e_fresh.sum(axis=-1)  10.5 us
    dot_general x8, matrix products, absorb(): jnp.einsum('kgts,skd->kgtd', e_fresh.astype(jnp.bfloat16), value_new, pre...  8.78 us
  transfers between devices with their start and end apart: 31, of which 16 were waited for; matrix products, arithmetic and copies ran while one was open for 0% of the time, Pallas kernels for 0%

commit v1 on v0

v1 whole, which is shorter than its diff:
```python
import functools
import math

import jax
import jax.numpy as jnp
from jax import lax
from jax.experimental import pallas as pl
from jax.experimental.pallas import tpu as pltpu
from jax.sharding import PartitionSpec as P

MESH = pl.DeviceIdType.MESH
NEG = -1e30
CH = 256
BF = jnp.bfloat16
F32 = jnp.float32


def attend_kernel(n, scale, plen, q, kc, vt, kn, vn, o_out, l_out,
                  kb, vb, vnb, qb, ob, lb, osend, lsend, s0, s1, mscr,
                  kvl, kvs, kvr, qls, qss, qrs, fss, oss, ors, lss, lrs):
    S = (s0, s1)
    heads, rows, dim = q.shape[1], q.shape[2], q.shape[3]
    cl, nl = kc.shape[2], kn.shape[2]
    cols = 2 * rows
    grp = rows // nl
    c2 = float(scale * math.log2(math.e))
    nch = n // 2
    me = lax.axis_index('cp')
    x, h = me // 2, lax.rem(me, 2)
    oh = 1 - h
    xl, xr, xd = lax.rem(x + nch - 1, nch), lax.rem(x + 1, nch), lax.rem(x + 2, nch)
    src_chip = (x, xl, xr, xd)

    def dev(chip, core):
        return {'cp': chip * 2 + core}

    def remote(src, dst, ss, rs, chip, core):
        return pltpu.make_async_remote_copy(src_ref=src, dst_ref=dst, send_sem=ss, recv_sem=rs,
                                            device_id=dev(chip, core), device_id_type=MESH)

    bar = pltpu.get_barrier_semaphore()
    for j in range(1, n):
        pl.semaphore_signal(bar, inc=1, device_id={'cp': lax.rem(me + j, n)}, device_id_type=MESH)

    def kv_parts(k, half, core):
        return ((kc.at[half, k], kb.at[k, pl.ds(pl.multiple_of(core * cl, 128), cl)]),
                (vt.at[half, k], vb.at[k, :, pl.ds(pl.multiple_of(core * cl, 128), cl)]),
                (kn.at[half, k], kb.at[k, pl.ds(pl.multiple_of(2 * cl + core * nl, 16), nl)]),
                (vn.at[half, k], vnb.at[k, pl.ds(pl.multiple_of(core * nl, 16), nl)]))

    def kv_local(k):
        return [pltpu.make_async_copy(s, d, kvl.at[k, i]) for i, (s, d) in enumerate(kv_parts(k, h, h))]

    def kv_remote(k):
        return [remote(s, d, kvs.at[k, i], kvr.at[k, i], x, oh) for i, (s, d) in enumerate(kv_parts(k, oh, h))]

    def q_local(k):
        return pltpu.make_async_copy(q.at[h, k], qb.at[0, k, pl.ds(pl.multiple_of(h * rows, 16), rows)], qls.at[k])

    def q_remote(k):
        out = []
        dst = pl.ds(pl.multiple_of(h * rows, 16), rows)
        i = 0
        for chip, rel in ((xl, 2), (xr, 1)):
            for core in (0, 1):
                out.append(remote(q.at[core, k], qb.at[rel, k, dst], qss.at[i, k], qrs.at[rel, h, k], chip, core))
                i += 1
        out.append(remote(q.at[oh, k], qb.at[0, k, dst], qss.at[i, k], qrs.at[0, h, k], x, oh))
        return out

    def q_arrive(rel, core, k):
        d = qb.at[rel, k, pl.ds(pl.multiple_of(core * rows, 16), rows)]
        return pltpu.make_async_copy(d, d, qrs.at[rel, core, k])

    def forward(k, way):
        rel, chip = ((1, xr), (2, xl))[way]
        piece = pl.ds(way * rows, rows)
        return remote(qb.at[rel, k, piece], qb.at[3, k, piece], fss.at[way, k], qrs.at[3, way, k], chip, h)

    for k in range(heads):
        for cp in kv_local(k):
            cp.start()
        q_local(k).start()
    pl.semaphore_wait(bar, n - 1)
    for k in range(heads):
        for cp in q_remote(k):
            cp.start()
        for cp in kv_remote(k):
            cp.start()

    def wait_kv(k):
        for cp in kv_local(k):
            cp.wait()
        for i, (s, d) in enumerate(kv_parts(k, h, oh)):
            pltpu.make_async_copy(d, d, kvr.at[k, i]).wait()

    def wait_q(k, c):
        if c == 0:
            q_local(k).wait()
            q_arrive(0, oh, k).wait()
        else:
            q_arrive(c, 0, k).wait()
            q_arrive(c, 1, k).wait()

    nkeys = 2 * cl + 2 * nl
    bounds = [(a, min(a + CH, 2 * cl)) for a in range(0, 2 * cl, CH)] + [(2 * cl, nkeys)]
    pref = plen[0] - x * (2 * cl)

    def score_chunk(k, qv, c, a, e, dst, mx):
        s = lax.dot_general(kb[k, a:e, :], qv, (((1,), (1,)), ((), ())), preferred_element_type=F32)
        if a < 2 * cl:
            seen = (lax.broadcasted_iota(jnp.int32, (e - a, 1), 0) + a) < pref
            s = jnp.where(seen, s, NEG)
        else:
            key = lax.broadcasted_iota(jnp.int32, (e - a, cols), 0) + x * (2 * nl)
            tok = lax.broadcasted_iota(jnp.int32, (e - a, cols), 1) // grp + src_chip[c] * (2 * nl)
            s = jnp.where(key <= tok, s, NEG)
        dst[a:e, :] = s
        mb = jnp.max(s.reshape((e - a) // 8, 8, cols), axis=0)
        return mb if mx is None else jnp.maximum(mx, mb)

    def value_chunk(k, a, e, srcs, mc, o, l):
        s = srcs[a:e, :]
        p = jnp.exp2(s * c2 - mc)
        lsum = jnp.sum(p.reshape((e - a) // 8, 8, cols), axis=0)
        vv = vb[k, :, a:e] if a < 2 * cl else vnb[k].T
        oo = jnp.dot(vv, p.astype(BF), preferred_element_type=F32)
        return (oo if o is None else o + oo), (lsum if l is None else l + lsum)

    def close_scores(slot, mx):
        mscr[slot] = jnp.broadcast_to(jnp.max(mx, axis=0, keepdims=True) * c2, (8, cols))

    def close_values(k, c, slot, o, l):
        u = k * 4 + c
        ls = jnp.sum(l, axis=0, keepdims=True)
        on = (o * (1.0 / ls)).T.astype(BF)
        osend[u] = on
        lsend[u] = mscr[slot][0:1, :] + jnp.log2(ls)

    def o_copies(k, c, a, core_static=None):
        u = k * 4 + c
        rel = (0, 2, 1, 3)[c]
        hh = h * heads + k
        return (remote(osend.at[u, pl.ds(pl.multiple_of(a * rows, 16), rows)], ob.at[rel, hh], oss.at[u, a], ors.at[rel, hh],
                       src_chip[c], a),
                remote(lsend.at[u], lb.at[rel, hh], lss.at[u, a], lrs.at[rel, hh], src_chip[c], a))

    def send_unit(k, c):
        if c == 0:
            for cp in o_copies(k, 0, oh):
                cp.start()
        else:
            for a in (0, 1):
                for cp in o_copies(k, c, a):
                    cp.start()

    def step(k, c, nxt):
        slot = c % 2
        mc = mscr[slot][0:1, :]
        mx = o = l = None
        if nxt is not None:
            k2, cc2 = nxt
            qv = qb[cc2, k2]
        for a, e in bounds:
            if nxt is not None:
                mx = score_chunk(k2, qv, cc2, a, e, S[1 - slot], mx)
            o, l = value_chunk(k, a, e, S[slot], mc, o, l)
        if nxt is not None:
            close_scores(1 - slot, mx)
        close_values(k, c, slot, o, l)

    def forwards(k):
        for way, rel in ((0, 1), (1, 2)):
            q_arrive(rel, way, k).wait()
            forward(k, way).start()

    def wait_q_rest(k, c):
        if c in (1, 2):
            q_arrive(c, 2 - c, k).wait()
        else:
            wait_q(k, c)

    wait_kv(0)
    wait_q(0, 0)
    mx = None
    q00 = qb[0, 0]
    for a, e in bounds:
        mx = score_chunk(0, q00, 0, a, e, s0, mx)
    close_scores(0, mx)
    forwards(0)

    def head_body(k, last):
        for c in range(4):
            if c < 3:
                wait_q_rest(k, c + 1)
                nxt = (k, c + 1)
            elif not last:
                wait_kv(k + 1)
                wait_q(k + 1, 0)
                nxt = (k + 1, 0)
            else:
                nxt = None
            if c == 2 and not last:
                forwards(k + 1)
            step(k, c, nxt)
            send_unit(k, c)

    def loop_body(k, carry):
        head_body(k, False)
        return carry

    lax.fori_loop(0, heads - 1, loop_body, 0)
    head_body(heads - 1, True)

    my = pl.ds(pl.multiple_of(h * rows, 16), rows)

    def own_l(hd_core, u):
        return None

    for hc in (0, 1):
        def comb(k, carry):
            hh = hc * heads + k

            @pl.when(hc != h)
            def _():
                d = ob.at[0, hh]
                pltpu.make_async_copy(d, d, ors.at[0, hh]).wait()
                d = lb.at[0, hh]
                pltpu.make_async_copy(d, d, lrs.at[0, hh]).wait()

            @pl.when(hc == h)
            def _():
                ob[0, hh] = osend[k * 4, my, :]
                lb[0, hh] = lsend[k * 4]

            for rel in (1, 2, 3):
                d = ob.at[rel, hh]
                pltpu.make_async_copy(d, d, ors.at[rel, hh]).wait()
                d = lb.at[rel, hh]
                pltpu.make_async_copy(d, d, lrs.at[rel, hh]).wait()
            ls = [lb[r, hh] for r in range(4)]
            ls = [jnp.where(h == 0, v[:, :rows], v[:, rows:]) for v in ls]
            m = jnp.maximum(jnp.maximum(ls[0], ls[1]), jnp.maximum(ls[2], ls[3]))
            w = [jnp.exp2(v - m) for v in ls]
            tot = (w[0] + w[1]) + (w[2] + w[3])
            inv = 1.0 / tot
            wt = jnp.concatenate([v * inv for v in w] + [jnp.zeros((4, rows), F32)], axis=0).T
            acc = None
            for r in range(4):
                t = ob[r, hh].astype(F32) * wt[:, r:r + 1]
                acc = t if acc is None else acc + t
            o_out[hh] = acc.astype(BF)
            l_out[hh] = (m + jnp.log2(tot)) * float(math.log(2.0))
            return carry
        lax.fori_loop(0, heads, comb, 0)

    def drain(k, carry):
        for cp in q_remote(k):
            cp.wait_send()
        for cp in kv_remote(k):
            cp.wait_send()
        for way in (0, 1):
            forward(k, way).wait_send()
        for c in range(4):
            if c == 0:
                for cp in o_copies(k, 0, oh):
                    cp.wait_send()
            else:
                for a in (0, 1):
                    for cp in o_copies(k, c, a):
                        cp.wait_send()
        return carry
    lax.fori_loop(0, heads, drain, 0)


def solution(mesh):
    n = mesh.shape['cp']
    tok = P(('dp', 'cp'))

    def local(queries, key_new, value_new, key_cache, value_cache, prefix_len):
        t, qh, d = queries.shape
        cl, kh = key_cache.shape[0], key_cache.shape[1]
        g = qh // kh
        hv = kh // 2
        rows = t * g
        nkeys = 2 * cl + 2 * t
        q = queries.reshape(t, kh, g, d).transpose(1, 0, 2, 3).reshape(2, hv, rows, d)
        kc = key_cache.transpose(1, 0, 2).reshape(2, hv, cl, d)
        vt = value_cache.transpose(1, 2, 0).reshape(2, hv, d, cl)
        kn = key_new.transpose(1, 0, 2).reshape(2, hv, t, d)
        vn = value_new.transpose(1, 0, 2).reshape(2, hv, t, d)
        anyspec = pl.BlockSpec(memory_space=pl.ANY)
        vm = pl.BlockSpec(memory_space=pltpu.VMEM)
        dma = pltpu.SemaphoreType.DMA
        o, l = pl.pallas_call(
            functools.partial(attend_kernel, n, d ** -0.5),
            name='attend',
            out_shape=(jax.ShapeDtypeStruct((kh, rows, d), BF), jax.ShapeDtypeStruct((kh, 1, rows), F32)),
            in_specs=[pl.BlockSpec(memory_space=pltpu.SMEM)] + [anyspec] * 5,
            out_specs=(vm, vm),
            scratch_shapes=[
                pltpu.VMEM((hv, nkeys, d), BF),
                pltpu.VMEM((hv, d, 2 * cl), BF),
                pltpu.VMEM((hv, 2 * t, d), BF),
                pltpu.VMEM((4, hv, 2 * rows, d), BF),
                pltpu.VMEM((4, kh, rows, d), BF),
                pltpu.VMEM((4, kh, 1, 2 * rows), F32),
                pltpu.VMEM((4 * hv, 2 * rows, d), BF),
                pltpu.VMEM((4 * hv, 1, 2 * rows), F32),
                pltpu.VMEM((nkeys, 2 * rows), F32),
                pltpu.VMEM((nkeys, 2 * rows), F32),
                pltpu.VMEM((2, 8, 2 * rows), F32),
                dma((hv, 4)), dma((hv, 4)), dma((hv, 4)),
                dma((hv,)), dma((5, hv)), dma((4, 2, hv)), dma((2, hv)),
                dma((4 * hv, 2)), dma((4, kh)), dma((4 * hv, 2)), dma((4, kh)),
            ],
            compiler_params=pltpu.CompilerParams(collective_id=0, has_side_effects=True,
                                                 vmem_limit_bytes=60 * 2 ** 20),
        )(prefix_len, q, kc, vt, kn, vn)
        attn = o.reshape(kh, t, g, d).transpose(1, 0, 2, 3).reshape(t, qh, d)
        lse = l.reshape(kh, t, g).transpose(1, 0, 2).reshape(t, qh)
        return attn, lse

    return jax.shard_map(local, mesh=mesh, in_specs=(tok, tok, tok, tok, tok, P('dp')), out_specs=(tok, tok), check_vma=False)
```

time: 257 us -> 65.6 us (0.26)
  the two profiles are of different devices: /device:TPU:112 before, /device:TPU:113 now
where the time goes in v1:
time: 65.6 us; the launch traced here: 65.4 us
  Pallas kernels  48.2 us (73%)
  local copies, waits for them, and re-layouts  15.8 us (24%)
  between operations  1.3 us (2%)
    pallas_call x1, Pallas kernels, local(): pl.pallas_call(functools.partial(attend_kernel, n, d ** (-0.5)), name='at...  48.2 us
    transpose x1, local copies, waits for them, and re-layouts, local(): kc = key_cache.transpose(1, 0, 2).reshape(2, hv, cl, d)  4.1 us
    transpose x1, local copies, waits for them, and re-layouts, local(): vt = value_cache.transpose(1, 2, 0).reshape(2, hv, d, cl)  3.36 us
    transpose x1, local copies, waits for them, and re-layouts, local(): attn = o.reshape(kh, t, g, d).transpose(1, 0, 2, 3).reshape(t, qh, d)  1.88 us
    reshape x1, local copies, waits for them, and re-layouts, local(): queries.reshape(t, kh, g, d).transpose(1, 0, 2, 3).reshape(2, hv, rows, d)  1.88 us
    transpose x1, local copies, waits for them, and re-layouts, local(): kn = key_new.transpose(1, 0, 2).reshape(2, hv, t, d)  1.55 us
    transpose x1, local copies, waits for them, and re-layouts, local(): vn = value_new.transpose(1, 0, 2).reshape(2, hv, t, d)  1.54 us

profile of v1, /device:TPU:113, one launch (start us, length us, event | category | flops | bytes accessed | tf_op | source)
XLA Modules:
  0.0 65.4 jit_solution(8661319062605814216)
XLA Ops:
  1.3 1.5 %copy.25 = bf16[8,48,128]{2,1,0:T(8,128)(2,1)} copy(bf16[8,48,128]{2,0,1:T(8,128)(2,1)} %bitcast.31) | data formatting | bytes 196608 | tf_op jit(solution)/shard_map/transpose | solution.py:290
  2.8 1.5 %copy.26 = bf16[8,48,128]{2,1,0:T(8,128)(2,1)} copy(bf16[8,48,128]{2,0,1:T(8,128)(2,1)} %bitcast.32) | data formatting | bytes 196608 | tf_op jit(solution)/shard_map/transpose | solution.py:291
  4.4 1.9 %copy.22 = bf16[48,8,4,128]{3,2,0,1:T(4,128)(2,1)} copy(bf16[48,8,4,128]{3,2,1,0:T(4,128)(2,1)} %bitcast.25) | data formatting | bytes 786432 | tf_op jit(solution)/shard_map/reshape | solution.py:287
  6.2 0.0 copy-start
  6.2 4.1 %copy.23 = bf16[8,1536,128]{2,1,0:T(8,128)(2,1)} copy(bf16[8,1536,128]{2,0,1:T(8,128)(2,1)} %bitcast.22) | data formatting | bytes 6291456 | tf_op jit(solution)/shard_map/transpose | solution.py:288
  10.3 0.0 copy-done
  10.3 3.4 %copy.24 = bf16[8,128,1536]{2,1,0:T(8,128)(2,1)} copy(bf16[8,128,1536]{1,0,2:T(8,128)(2,1)S(1)} %bitcast.23) | data formatting | bytes 6291456 | tf_op jit(solution)/shard_map/transpose | solution.py:289
  13.7 48.2 %attend.1 = (bf16[8,192,128]{2,1,0:T(8,128)(2,1)}, f32[8,1,192]{2,1,0:T(1,128)}) custom-call(s32[1]{0:T(128)S(6)} %copy.30.plen, bf16[2,4,192,128]{3,2,1,0:T(8,128)(2,1)} %bitcast.24, bf16[2,4,1536,128]{3,2,1,0:T(8,128)(2,1)} %bitcast.20, bf16[2,4,128,1536]{3,2,1,0:T(8,128)(2,1)} %bitcast.21, bf16[2,4,48,128]{3,2,1,0:T(8,128)(2,1)} %bitcast.29, ...), custom_call_target="tpu_custom_call" | custom-call | tf_op jit(solution)/shard_map/attend/pallas_call | solution.py:295
  62.0 1.9 %copy.27 = bf16[48,8,4,128]{3,2,1,0:T(4,128)(2,1)} copy(bf16[48,8,4,128]{3,2,0,1:T(4,128)(2,1)} %bitcast.27) | data formatting | bytes 786432 | tf_op jit(solution)/shard_map/transpose | solution.py:320
  63.8 0.8 %copy.28 = f32[8,1,192]{0,2,1:T(8,128)S(1)} copy(f32[8,1,192]{2,1,0:T(1,128)} %get-tuple-element.5) | data formatting | bytes 12288 | tf_op jit(solution)/shard_map/attend/pallas_call | solution.py:295
  64.7 0.7 %copy.29 = f32[48,8,4]{0,2,1:T(4,128)} copy(f32[48,8,4]{1,2,0:T(4,128)S(1)} %bitcast.28) | data formatting | bytes 12288 | tf_op jit(solution)/shard_map/transpose | solution.py:321
Async XLA Ops:
  6.2 4.1 %copy-start = (bf16[1536,8,128]{2,1,0:T(8,128)(2,1)S(1)}, bf16[1536,8,128]{2,1,0:T(8,128)(2,1)}, u32[]{:S(2)}) copy-start(bf16[1536,8,128]{2,1,0:T(8,128)(2,1)} %param.10) | copy-start | bytes 9437188

commit v2 on v0

v2 whole, which is shorter than its diff:
```python
import functools
import math

import jax
import jax.numpy as jnp
from jax import lax
from jax.experimental import pallas as pl
from jax.experimental.pallas import tpu as pltpu
from jax.sharding import PartitionSpec as P

MESH = pl.DeviceIdType.MESH
NEG = -1e30
CH = 256
PREP = 256
PARTS = 3
BF = jnp.bfloat16
F32 = jnp.float32
LEFT, RIGHT, FAR = 1, 2, 3
UNITS = ((0, LEFT), (0, RIGHT), (1, LEFT), (1, RIGHT), (0, FAR), (1, FAR),
         (2, LEFT), (2, RIGHT), (2, FAR), (3, FAR), (3, LEFT), (3, RIGHT))


def pick(i, table):
    out = table[0]
    for j, v in enumerate(table[1:], 1):
        out = jnp.where(i == j, v, out)
    return out


def attend_kernel(n, scale, plen, q, kn, vn, kc, vc, o_out, l_out,
                  kb, vb, kst, vst, knst, vnst, prep, qb, ob, lb, osend, lsend, orel, lrel, s0, s1, mscr, lfin,
                  kvl, kvs, kvr, nvl, nvs, nvr, qss, qrs, fss, oss, ors, lss, lrs, rss, rrs, rls, rlr):
    S = (s0, s1)
    toks, heads, grp, dim = q.shape[0], q.shape[2], q.shape[3], q.shape[4]
    rows = toks * grp
    cols = 2 * rows
    cl = kc.shape[0]
    c2 = float(scale * math.log2(math.e))
    nch = n // 2
    me = lax.axis_index('cp')
    x, h = me // 2, lax.rem(me, 2)
    oh = 1 - h
    xl, xr, xd = lax.rem(x + nch - 1, nch), lax.rem(x + 1, nch), lax.rem(x + 2, nch)
    chips = (x, xl, xr, xd)

    def chip_of(c):
        return chips[c] if isinstance(c, int) else pick(c, chips)

    def remote(src, dst, ss, rs, chip, core):
        return pltpu.make_async_remote_copy(src_ref=src, dst_ref=dst, send_sem=ss, recv_sem=rs,
                                            device_id={'cp': chip * 2 + core}, device_id_type=MESH)

    def arrived(dst, sem):
        pltpu.make_async_copy(dst, dst, sem).wait()

    bar = pltpu.get_barrier_semaphore()
    for j in range(1, n):
        pl.semaphore_signal(bar, inc=1, device_id={'cp': lax.rem(me + j, n)}, device_id_type=MESH)

    part = cl // PARTS

    def kv_local(p):
        src = pl.ds(p * part, part)
        return [pltpu.make_async_copy(a.at[src, h], st.at[src], kvl.at[i, p]) for i, (a, st) in enumerate(((kc, kst), (vc, vst)))]

    def kv_remote(p):
        src, dst = pl.ds(p * part, part), pl.ds(cl + p * part, part)
        return [remote(a.at[src, oh], st.at[dst], kvs.at[i, p], kvr.at[i, p], x, oh) for i, (a, st) in enumerate(((kc, kst), (vc, vst)))]

    def kv_arrived(p):
        dst = pl.ds(cl + p * part, part)
        for i, st in enumerate((kst, vst)):
            arrived(st.at[dst], kvr.at[i, p])

    nrow = pl.ds(h * toks, toks)

    def new_local():
        return [pltpu.make_async_copy(a.at[:, h], st.at[nrow], nvl.at[i]) for i, (a, st) in enumerate(((kn, knst), (vn, vnst)))]

    def new_remote():
        return [remote(a.at[:, oh], st.at[nrow], nvs.at[i], nvr.at[i], x, oh) for i, (a, st) in enumerate(((kn, knst), (vn, vnst)))]

    def q_local(k):
        return pltpu.make_async_copy(q.at[:, h, k], qb.at[0, k, nrow], qrs.at[0, h, k])

    def q_partner(k):
        return remote(q.at[:, oh, k], qb.at[0, k, nrow], qss.at[4, k], qrs.at[0, h, k], x, oh)

    def q_remote(k):
        out = []
        for chip, rel in ((xl, RIGHT), (xr, LEFT)):
            for core in (0, 1):
                out.append(remote(q.at[:, core, k], qb.at[rel, k, nrow], qss.at[len(out), k], qrs.at[rel, h, k], chip, core))
        return out

    def q_arrived(rel, core, k):
        arrived(qb.at[rel, k, pl.ds(core * toks, toks)], qrs.at[rel, core, k])

    def forward(k, way):
        rel, chip = ((LEFT, xr), (RIGHT, xl))[way]
        piece = pl.ds(way * toks, toks)
        return remote(qb.at[rel, k, piece], qb.at[FAR, k, piece], fss.at[way, k], qrs.at[FAR, way, k], chip, h)

    def forwards(k):
        for way, rel in ((0, LEFT), (1, RIGHT)):
            q_arrived(rel, way, k)
            forward(k, way).start()

    for p in range(PARTS):
        for cp in kv_local(p):
            cp.start()
    for cp in new_local():
        cp.start()
    for k in range(heads):
        q_local(k).start()
    pl.semaphore_wait(bar, n - 1)
    for k in range(heads):
        q_partner(k).start()
    for cp in new_remote():
        cp.start()
    for k in range(heads):
        for cp in q_remote(k):
            cp.start()
    for p in range(PARTS):
        for cp in kv_remote(p):
            cp.start()

    def split(kraw, vraw, count, base):
        prep[0, 0:count * heads] = kraw.reshape(count * heads, dim).astype(F32)
        prep[1, 0:count * heads] = vraw.reshape(count * heads, dim).astype(F32)
        for j in range(heads):
            kb[j, pl.ds(base, count), :] = prep[0, pl.ds(j, count, stride=heads), :].astype(BF)
            vb[j, :, pl.ds(base, count)] = prep[1, pl.ds(j, count, stride=heads), :].astype(BF).T

    def split_part(first):
        def go(i, carry):
            base = pl.multiple_of(first + i * PREP, PREP)
            split(kst[pl.ds(base, PREP)], vst[pl.ds(base, PREP)], PREP, base)
            return carry
        lax.fori_loop(0, part // PREP, go, 0)

    pref = plen[0] - x * (2 * cl)
    own_b = [(a, a + CH) for a in range(0, cl, CH)]
    oth_b = [(a, a + CH) for a in range(cl, 2 * cl, CH)]
    new_b = [(2 * cl, 2 * cl + 2 * toks)]
    all_b = own_b + oth_b + new_b

    def score_chunk(k, qv, chip, a, e, dst, mx):
        s = lax.dot_general(kb[k, a:e, :], qv, (((1,), (1,)), ((), ())), preferred_element_type=F32)
        if a < 2 * cl:
            first = h * cl + a if a < cl else oh * cl + (a - cl)
            s = jnp.where(lax.broadcasted_iota(jnp.int32, (e - a, 1), 0) < pref - first, s, NEG)
        else:
            key = lax.broadcasted_iota(jnp.int32, (e - a, cols), 0)
            tok = lax.broadcasted_iota(jnp.int32, (e - a, cols), 1) // grp
            s = jnp.where(key - tok <= (chip - x) * (2 * toks), s, NEG)
        dst[a:e, :] = s
        mb = jnp.max(s.reshape((e - a) // 8, 8, cols), axis=0)
        return mb if mx is None else jnp.maximum(mx, mb)

    def value_chunk(k, a, e, src, mc, o, l):
        p = jnp.exp2(src[a:e, :] * c2 - mc)
        lsum = jnp.sum(p.reshape((e - a) // 8, 8, cols), axis=0)
        oo = jnp.dot(vb[k, :, a:e], p.astype(BF), preferred_element_type=F32)
        return (oo if o is None else o + oo), (lsum if l is None else l + lsum)

    def step(slot, cur, nxt):
        mx = o = l = None
        if nxt is not None:
            k2, r2, b2 = nxt
            qv = qb[r2, k2].reshape(cols, dim)
            chip = chip_of(r2)
        if cur is not None:
            k, b1, u = cur
            mc = mscr[slot][0:1, :]
        for i in range(max(len(b2) if nxt is not None else 0, len(b1) if cur is not None else 0)):
            if nxt is not None and i < len(b2):
                mx = score_chunk(k2, qv, chip, *b2[i], S[1 - slot], mx)
            if cur is not None and i < len(b1):
                o, l = value_chunk(k, *b1[i], S[slot], mc, o, l)
        if nxt is not None:
            mscr[1 - slot] = jnp.broadcast_to(jnp.max(mx, axis=0, keepdims=True) * c2, (8, cols))
        if cur is not None:
            ls = jnp.sum(l, axis=0, keepdims=True)
            osend[u] = (o * (1.0 / ls)).T.astype(BF)
            lse = mc + jnp.log2(ls)
            lsend[u, 0] = lse[:, :rows]
            lsend[u, 1] = lse[:, rows:]

    def slot_of(k, c):
        return k * 3 + (c - 1)

    def own_slot(k, half):
        return heads * 3 + half * heads + k

    def piece(a):
        return pl.ds(pl.multiple_of(a * rows, 16), rows)

    def result(u, a, dst_o, dst_l, so, sl, chip, core):
        return (remote(osend.at[u, piece(a)], dst_o, oss.at[u, a], so, chip, core),
                remote(lsend.at[u, a], dst_l, lss.at[u, a], sl, chip, core))

    hh_of = lambda k: h * heads + k

    def own_copies(k, half):
        hh = hh_of(k)
        rel = 3 * half
        return result(own_slot(k, half), oh, ob.at[rel, hh], lb.at[rel, hh], ors.at[rel, hh], lrs.at[rel, hh], x, oh)

    def side_copies(k, c):
        hh = hh_of(k)
        if isinstance(c, int):
            a, rel, chip = (c - 1), 3 - c, chips[c]
        else:
            a, rel, chip = c - 1, 3 - c, pick(c, chips)
        return result(slot_of(k, c), a, ob.at[rel, hh], lb.at[rel, hh], ors.at[rel, hh], lrs.at[rel, hh], chip, a)

    def far_copies(k, a):
        chip = (xr, xl)[a]
        return result(slot_of(k, FAR), a, orel.at[a, k], lrel.at[a, k], rrs.at[a, k], rlr.at[a, k], chip, h)

    def merged_copies(k, a):
        hh = hh_of(k)
        chip, rel = ((xr, LEFT), (xl, RIGHT))[a]
        return (remote(orel.at[a, heads + k], ob.at[rel, hh], rss.at[a, k], ors.at[rel, hh], chip, a),
                remote(lrel.at[a, heads + k], lb.at[rel, hh], rls.at[a, k], lrs.at[rel, hh], chip, a))

    def columns(ws):
        pad = jnp.zeros((8 - len(ws), rows), F32)
        return jnp.concatenate(list(ws) + [pad], axis=0).T

    def relay(k):
        for a in (0, 1):
            arrived(orel.at[a, k], rrs.at[a, k])
            arrived(lrel.at[a, k], rlr.at[a, k])
        for a in (0, 1):
            u = slot_of(k, (RIGHT, LEFT)[a])
            l0, l1 = lsend[u, a], lrel[a, k]
            m = jnp.maximum(l0, l1)
            w0, w1 = jnp.exp2(l0 - m), jnp.exp2(l1 - m)
            tot = w0 + w1
            inv = 1.0 / tot
            wt = columns((w0 * inv, w1 * inv))
            orel[a, heads + k] = (osend[u, a * rows:(a + 1) * rows, :].astype(F32) * wt[:, 0:1]
                                  + orel[a, k].astype(F32) * wt[:, 1:2]).astype(BF)
            lrel[a, heads + k] = m + jnp.log2(tot)
        for a in (0, 1):
            for cp in merged_copies(k, a):
                cp.start()

    def start(cps):
        for cp in cps:
            cp.start()

    def wait_q(k, c):
        if isinstance(c, int):
            if c != LEFT:
                q_arrived(c, 0, k)
            if c != RIGHT:
                q_arrived(c, 1, k)
        else:
            @pl.when(c != LEFT)
            def _():
                q_arrived(c, 0, k)

            @pl.when(c != RIGHT)
            def _():
                q_arrived(c, 1, k)

    def send_unit(k, c):
        if isinstance(c, int):
            if c == FAR:
                start(far_copies(k, 0))
                start(far_copies(k, 1))
            else:
                start(side_copies(k, c))
        else:
            @pl.when(c == FAR)
            def _():
                start(far_copies(k, 0))
                start(far_copies(k, 1))

            @pl.when(c != FAR)
            def _():
                start(side_copies(k, c))

    for p in range(PARTS):
        for cp in kv_local(p):
            cp.wait()
        split_part(p * part)
    wait_q(0, 0)
    step(1, None, (0, 0, own_b))
    for k in range(heads):
        if k + 1 < heads:
            wait_q(k + 1, 0)
        step(k % 2, (k, own_b, own_slot(k, 0)), (k + 1, 0, own_b) if k + 1 < heads else None)
        start(own_copies(k, 0))
        if k == 1:
            forwards(0)
    forwards(1)

    for cp in new_local():
        cp.wait()
    for i, st in enumerate((knst, vnst)):
        arrived(st.at[pl.ds(oh * toks, toks)], nvr.at[i])
    split(knst[...], vnst[...], 2 * toks, 2 * cl)
    for p in range(PARTS):
        kv_arrived(p)
        split_part(cl + p * part)
    forwards(2)

    def go(u, k, c, k2, c2_, slot):
        wait_q(k2, c2_)
        step(slot, (k, all_b, slot_of(k, c)), (k2, c2_, all_b))
        send_unit(k, c)

    hs, cs = [u[0] for u in UNITS], [u[1] for u in UNITS]
    wait_q(*UNITS[0])
    step(1, None, UNITS[0] + (all_b,))

    def pair(i, carry):
        u = 2 * i
        go(u, pick(u, hs), pick(u, cs), pick(u + 1, hs), pick(u + 1, cs), 0)

        @pl.when(i == 0)
        def _():
            forwards(3)
        go(u + 1, pick(u + 1, hs), pick(u + 1, cs), pick(u + 2, hs), pick(u + 2, cs), 1)

        @pl.when(i == 3)
        def _():
            relay(0)
            relay(1)
        return carry

    lax.fori_loop(0, len(UNITS) // 2 - 1, pair, 0)
    k, c = UNITS[-2]
    k2, c2_ = UNITS[-1]
    wait_q(k2, c2_)
    step(0, (k, all_b, slot_of(k, c)), (k2, c2_, all_b))
    send_unit(k, c)
    relay(2)
    rest = oth_b + new_b
    step(1, (k2, all_b, slot_of(k2, c2_)), (0, 0, rest))
    send_unit(k2, c2_)
    relay(3)

    for k in range(heads):
        step(k % 2, (k, rest, own_slot(k, 1)), (k + 1, 0, rest) if k + 1 < heads else None)
        start(own_copies(k, 1))

    def final(k, own):
        hh = (h if own else oh) * heads + k
        if own:
            parts = [(osend[own_slot(k, half), piece(h), :], lsend[own_slot(k, half), h]) for half in (0, 1)]
        else:
            for rel in (0, 3):
                arrived(ob.at[rel, hh], ors.at[rel, hh])
                arrived(lb.at[rel, hh], lrs.at[rel, hh])
            parts = [(ob[rel, hh], lb[rel, hh]) for rel in (0, 3)]
        parts += [(ob[rel, hh], lb[rel, hh]) for rel in (LEFT, RIGHT)]
        ls = [p[1] for p in parts]
        m = jnp.maximum(jnp.maximum(ls[0], ls[1]), jnp.maximum(ls[2], ls[3]))
        w = [jnp.exp2(v - m) for v in ls]
        tot = (w[0] + w[1]) + (w[2] + w[3])
        inv = 1.0 / tot
        wt = columns([v * inv for v in w])
        acc = None
        for r in range(4):
            t = parts[r][0].astype(F32) * wt[:, r:r + 1]
            acc = t if acc is None else acc + t
        o_out[:, hh] = acc.astype(BF).reshape(toks, grp, dim)
        lfin[pl.ds(hh, 1), :] = (m + jnp.log2(tot)) * float(math.log(2.0))

    for k in range(heads):
        for own in (True, False):
            hh = (h if own else oh) * heads + k
            for rel in (LEFT, RIGHT):
                arrived(ob.at[rel, hh], ors.at[rel, hh])
                arrived(lb.at[rel, hh], lrs.at[rel, hh])
        for own in (True, False):
            final(k, own)
    l_out[...] = lfin[...]

    def drain(k, carry):
        cps = list(q_remote(k)) + [q_partner(k), forward(k, 0), forward(k, 1)]
        for half in (0, 1):
            cps += own_copies(k, half)
        for c in (LEFT, RIGHT):
            cps += side_copies(k, c)
        for a in (0, 1):
            cps += far_copies(k, a)
            cps += merged_copies(k, a)
        for cp in cps:
            cp.wait_send()
        return carry
    lax.fori_loop(0, heads, drain, 0)
    for cp in new_remote():
        cp.wait_send()
    for p in range(PARTS):
        for cp in kv_remote(p):
            cp.wait_send()


def solution(mesh):
    n = mesh.shape['cp']
    tok = P(('dp', 'cp'))

    def local(queries, key_new, value_new, key_cache, value_cache, prefix_len):
        t, qh, d = queries.shape
        cl, kh = key_cache.shape[0], key_cache.shape[1]
        g = qh // kh
        hv = kh // 2
        rows = t * g
        nkeys = 2 * cl + 2 * t
        width = -(-nkeys // 128) * 128
        q = queries.reshape(t, 2, hv, g, d)
        kc, vc = (a.reshape(cl, 2, hv, d) for a in (key_cache, value_cache))
        kn, vn = (a.reshape(t, 2, hv, d) for a in (key_new, value_new))
        anyspec = pl.BlockSpec(memory_space=pl.ANY)
        vm = pl.BlockSpec(memory_space=pltpu.VMEM)
        dma = pltpu.SemaphoreType.DMA
        nres = 5 * hv
        o, l = pl.pallas_call(
            functools.partial(attend_kernel, n, d ** -0.5),
            name='attend',
            out_shape=(jax.ShapeDtypeStruct((t, kh, g, d), BF), jax.ShapeDtypeStruct((kh, rows), F32)),
            in_specs=[pl.BlockSpec(memory_space=pltpu.SMEM)] + [anyspec] * 5,
            out_specs=(vm, vm),
            scratch_shapes=[
                pltpu.VMEM((hv, nkeys, d), BF),
                pltpu.VMEM((hv, d, width), BF),
                pltpu.VMEM((2 * cl, hv, d), BF),
                pltpu.VMEM((2 * cl, hv, d), BF),
                pltpu.VMEM((2 * t, hv, d), BF),
                pltpu.VMEM((2 * t, hv, d), BF),
                pltpu.VMEM((2, PREP * hv, d), F32),
                pltpu.VMEM((4, hv, 2 * t, g, d), BF),
                pltpu.VMEM((4, kh, rows, d), BF),
                pltpu.VMEM((4, kh, 1, rows), F32),
                pltpu.VMEM((nres, 2 * rows, d), BF),
                pltpu.VMEM((nres, 2, 1, rows), F32),
                pltpu.VMEM((2, 2 * hv, rows, d), BF),
                pltpu.VMEM((2, 2 * hv, 1, rows), F32),
                pltpu.VMEM((nkeys, 2 * rows), F32),
                pltpu.VMEM((nkeys, 2 * rows), F32),
                pltpu.VMEM((2, 8, 2 * rows), F32),
                pltpu.VMEM((kh, rows), F32),
                dma((2, PARTS)), dma((2, PARTS)), dma((2, PARTS)),
                dma((2,)), dma((2,)), dma((2,)),
                dma((5, hv)), dma((4, 2, hv)), dma((2, hv)),
                dma((nres, 2)), dma((4, kh)), dma((nres, 2)), dma((4, kh)),
                dma((2, hv)), dma((2, hv)), dma((2, hv)), dma((2, hv)),
            ],
            compiler_params=pltpu.CompilerParams(collective_id=0, has_side_effects=True,
                                                 vmem_limit_bytes=62 * 2 ** 20),
        )(prefix_len, q, kn, vn, kc, vc)
        lse = l.reshape(kh, t, g).transpose(1, 0, 2).reshape(t, qh)
        return o.reshape(t, qh, d), lse

    return jax.shard_map(local, mesh=mesh, in_specs=(tok, tok, tok, tok, tok, P('dp')), out_specs=(tok, tok), check_vma=False)
```

time: 257 us -> 49.3 us (0.19)
  the two profiles are of different devices: /device:TPU:112 before, /device:TPU:113 now
where the time goes in v2:
time: 49.3 us; the launch traced here: 49.1 us
  Pallas kernels  44.5 us (90%)
  local copies, waits for them, and re-layouts  3.27 us (7%)
  between operations  1.3 us (3%)
    pallas_call x1, Pallas kernels, local(): pl.pallas_call(functools.partial(attend_kernel, n, d ** (-0.5)), name='at...  44.5 us
    unnamed x1, local copies, waits for them, and re-layouts  1.77 us

profile of v2, /device:TPU:113, one launch (start us, length us, event | category | flops | bytes accessed | tf_op | source)
XLA Modules:
  0.0 49.1 jit_solution(8714859832602632527)
XLA Ops:
  1.3 44.5 %attend.1 = (bf16[48,8,4,128]{3,2,1,0:T(4,128)(2,1)}, f32[8,192]{1,0:T(8,128)}) custom-call(s32[1]{0:T(128)S(6)} %copy.13.plen, bf16[48,2,4,4,128]{4,3,2,1,0:T(4,128)(2,1)} %bitcast.14, bf16[48,2,4,128]{3,2,1,0:T(4,128)(2,1)} %bitcast.15, bf16[48,2,4,128]{3,2,1,0:T(4,128)(2,1)} %bitcast.16, bf16[1536,2,4,128]{3,2,1,0:T(4,128)(2,1)} %bitcast.10, ...), custom_call_target="tpu_custom_call" | custom-call | tf_op jit(solution)/shard_map/attend/pallas_call | solution.py:424
  45.8 0.8 %copy.10 = f32[8,192]{0,1:T(8,128)S(1)} copy(f32[8,192]{1,0:T(8,128)} %get-tuple-element.5) | data formatting | bytes 12288 | tf_op jit(solution)/shard_map/attend/pallas_call | solution.py:424
  46.6 0.7 %copy.11 = f32[48,8,4]{0,2,1:T(4,128)} copy(f32[48,8,4]{1,2,0:T(4,128)S(1)} %bitcast.13) | data formatting | bytes 12288 | tf_op jit(solution)/shard_map/transpose | solution.py:458
  47.3 1.8 %copy.14 = bf16[48,32,128]{2,1,0:T(8,128)(2,1)} copy(bf16[48,32,128]{2,1,0:T(8,128)(2,1)} %bitcast.12) | data formatting | bytes 786432

commit v3 on v2

--- a/solution.py
+++ b/solution.py
@@ -13,6 +13,7 @@
 CH = 256
 PREP = 256
 PARTS = 3
+LOOPED = 8
 BF = jnp.bfloat16
 F32 = jnp.float32
 LEFT, RIGHT, FAR = 1, 2, 3
@@ -28,8 +29,8 @@
 
 
 def attend_kernel(n, scale, plen, q, kn, vn, kc, vc, o_out, l_out,
-                  kb, vb, kst, vst, knst, vnst, prep, qb, ob, lb, osend, lsend, orel, lrel, s0, s1, mscr, lfin,
-                  kvl, kvs, kvr, nvl, nvs, nvr, qss, qrs, fss, oss, ors, lss, lrs, rss, rrs, rls, rlr):
+                  kb, vb, kst, vst, knst, vnst, prep, qb, ob, lb, osend, lsend, orel, lrel, s0, s1, mscr, lfin, ltr,
+                  kvl, kvs, kvr, nvl, nvs, nvr, qss, qrs, oss, ors, lss, lrs, rss, rrs, rls, rlr):
     S = (s0, s1)
     toks, heads, grp, dim = q.shape[0], q.shape[2], q.shape[3], q.shape[4]
     rows = toks * grp
@@ -65,7 +66,7 @@
 
     def kv_remote(p):
         src, dst = pl.ds(p * part, part), pl.ds(cl + p * part, part)
-        return [remote(a.at[src, oh], st.at[dst], kvs.at[i, p], kvr.at[i, p], x, oh) for i, (a, st) in enumerate(((kc, kst), (vc, vst)))]
+        return [remote(a.at[src, oh], st.at[dst], kvs.at[i], kvr.at[i, p], x, oh) for i, (a, st) in enumerate(((kc, kst), (vc, vst)))]
 
     def kv_arrived(p):
         dst = pl.ds(cl + p * part, part)
@@ -81,25 +82,25 @@
         return [remote(a.at[:, oh], st.at[nrow], nvs.at[i], nvr.at[i], x, oh) for i, (a, st) in enumerate(((kn, knst), (vn, vnst)))]
 
     def q_local(k):
-        return pltpu.make_async_copy(q.at[:, h, k], qb.at[0, k, nrow], qrs.at[0, h, k])
+        return pltpu.make_async_copy(q.at[:, h, k], qb.at[k, nrow], qrs.at[0, h, k])
 
     def q_partner(k):
-        return remote(q.at[:, oh, k], qb.at[0, k, nrow], qss.at[4, k], qrs.at[0, h, k], x, oh)
+        return remote(q.at[:, oh, k], qb.at[k, nrow], qss, qrs.at[0, h, k], x, oh)
 
     def q_remote(k):
         out = []
         for chip, rel in ((xl, RIGHT), (xr, LEFT)):
             for core in (0, 1):
-                out.append(remote(q.at[:, core, k], qb.at[rel, k, nrow], qss.at[len(out), k], qrs.at[rel, h, k], chip, core))
+                out.append(remote(q.at[:, core, k], qb.at[rel * heads + k, nrow], qss, qrs.at[rel, h, k], chip, core))
         return out
 
     def q_arrived(rel, core, k):
-        arrived(qb.at[rel, k, pl.ds(core * toks, toks)], qrs.at[rel, core, k])
+        arrived(qb.at[rel * heads + k, pl.ds(core * toks, toks)], qrs.at[rel, core, k])
 
     def forward(k, way):
         rel, chip = ((LEFT, xr), (RIGHT, xl))[way]
         piece = pl.ds(way * toks, toks)
-        return remote(qb.at[rel, k, piece], qb.at[FAR, k, piece], fss.at[way, k], qrs.at[FAR, way, k], chip, h)
+        return remote(qb.at[rel * heads + k, piece], qb.at[FAR * heads + k, piece], qss, qrs.at[FAR, way, k], chip, h)
 
     def forwards(k):
         for way, rel in ((0, LEFT), (1, RIGHT)):
@@ -164,16 +165,19 @@
         oo = jnp.dot(vb[k, :, a:e], p.astype(BF), preferred_element_type=F32)
         return (oo if o is None else o + oo), (lsum if l is None else l + lsum)
 
-    def step(slot, cur, nxt):
+    def step(slot, cur, nxt, extra=None):
         mx = o = l = None
         if nxt is not None:
             k2, r2, b2 = nxt
-            qv = qb[r2, k2].reshape(cols, dim)
+            qv = qb[r2 * heads + k2].reshape(cols, dim)
             chip = chip_of(r2)
         if cur is not None:
             k, b1, u = cur
             mc = mscr[slot][0:1, :]
-        for i in range(max(len(b2) if nxt is not None else 0, len(b1) if cur is not None else 0)):
+        count = max(len(b2) if nxt is not None else 0, len(b1) if cur is not None else 0)
+        for i in range(count):
+            if extra is not None and i == count // 3:
+                extra()
             if nxt is not None and i < len(b2):
                 mx = score_chunk(k2, qv, chip, *b2[i], S[1 - slot], mx)
             if cur is not None and i < len(b1):
@@ -197,8 +201,8 @@
         return pl.ds(pl.multiple_of(a * rows, 16), rows)
 
     def result(u, a, dst_o, dst_l, so, sl, chip, core):
-        return (remote(osend.at[u, piece(a)], dst_o, oss.at[u, a], so, chip, core),
-                remote(lsend.at[u, a], dst_l, lss.at[u, a], sl, chip, core))
+        return (remote(osend.at[u, piece(a)], dst_o, oss, so, chip, core),
+                remote(lsend.at[u, a], dst_l, lss, sl, chip, core))
 
     hh_of = lambda k: h * heads + k
 
@@ -222,17 +226,19 @@
     def merged_copies(k, a):
         hh = hh_of(k)
         chip, rel = ((xr, LEFT), (xl, RIGHT))[a]
-        return (remote(orel.at[a, heads + k], ob.at[rel, hh], rss.at[a, k], ors.at[rel, hh], chip, a),
-                remote(lrel.at[a, heads + k], lb.at[rel, hh], rls.at[a, k], lrs.at[rel, hh], chip, a))
+        return (remote(orel.at[a, heads + k], ob.at[rel, hh], rss, ors.at[rel, hh], chip, a),
+                remote(lrel.at[a, heads + k], lb.at[rel, hh], rls, lrs.at[rel, hh], chip, a))
 
     def columns(ws):
         pad = jnp.zeros((8 - len(ws), rows), F32)
         return jnp.concatenate(list(ws) + [pad], axis=0).T
 
-    def relay(k):
+    def relay_wait(k):
         for a in (0, 1):
             arrived(orel.at[a, k], rrs.at[a, k])
             arrived(lrel.at[a, k], rlr.at[a, k])
+
+    def relay_merge(k):
         for a in (0, 1):
             u = slot_of(k, (RIGHT, LEFT)[a])
             l0, l1 = lsend[u, a], lrel[a, k]
@@ -244,6 +250,8 @@
             orel[a, heads + k] = (osend[u, a * rows:(a + 1) * rows, :].astype(F32) * wt[:, 0:1]
                                   + orel[a, k].astype(F32) * wt[:, 1:2]).astype(BF)
             lrel[a, heads + k] = m + jnp.log2(tot)
+
+    def relay_send(k):
         for a in (0, 1):
             for cp in merged_copies(k, a):
                 cp.start()
@@ -290,14 +298,12 @@
         split_part(p * part)
     wait_q(0, 0)
     step(1, None, (0, 0, own_b))
-    for k in range(heads):
-        if k + 1 < heads:
-            wait_q(k + 1, 0)
-        step(k % 2, (k, own_b, own_slot(k, 0)), (k + 1, 0, own_b) if k + 1 < heads else None)
+    for k in range(heads - 1):
+        wait_q(k + 1, 0)
+        step(k % 2, (k, own_b, own_slot(k, 0)), (k + 1, 0, own_b))
         start(own_copies(k, 0))
         if k == 1:
             forwards(0)
-    forwards(1)
 
     for cp in new_local():
         cp.wait()
@@ -307,7 +313,10 @@
     for p in range(PARTS):
         kv_arrived(p)
         split_part(cl + p * part)
-    forwards(2)
+    forwards(1)
+    wait_q(*UNITS[0])
+    step((heads - 1) % 2, (heads - 1, own_b, own_slot(heads - 1, 0)), UNITS[0] + (all_b,))
+    start(own_copies(heads - 1, 0))
 
     def go(u, k, c, k2, c2_, slot):
         wait_q(k2, c2_)
@@ -315,48 +324,39 @@
         send_unit(k, c)
 
     hs, cs = [u[0] for u in UNITS], [u[1] for u in UNITS]
-    wait_q(*UNITS[0])
-    step(1, None, UNITS[0] + (all_b,))
 
     def pair(i, carry):
         u = 2 * i
         go(u, pick(u, hs), pick(u, cs), pick(u + 1, hs), pick(u + 1, cs), 0)
 
-        @pl.when(i == 0)
+        @pl.when(i < 2)
         def _():
-            forwards(3)
+            forwards(2 + i)
         go(u + 1, pick(u + 1, hs), pick(u + 1, cs), pick(u + 2, hs), pick(u + 2, cs), 1)
-
-        @pl.when(i == 3)
-        def _():
-            relay(0)
-            relay(1)
         return carry
 
-    lax.fori_loop(0, len(UNITS) // 2 - 1, pair, 0)
-    k, c = UNITS[-2]
-    k2, c2_ = UNITS[-1]
-    wait_q(k2, c2_)
-    step(0, (k, all_b, slot_of(k, c)), (k2, c2_, all_b))
-    send_unit(k, c)
-    relay(2)
+    lax.fori_loop(0, LOOPED // 2, pair, 0)
     rest = oth_b + new_b
-    step(1, (k2, all_b, slot_of(k2, c2_)), (0, 0, rest))
-    send_unit(k2, c2_)
-    relay(3)
-
-    for k in range(heads):
-        step(k % 2, (k, rest, own_slot(k, 1)), (k + 1, 0, rest) if k + 1 < heads else None)
-        start(own_copies(k, 1))
+    last = len(UNITS) - 1
+    relays = {LOOPED: 0, LOOPED + 1: 1, LOOPED + 2: 2}
+    for u in range(LOOPED, last + 1):
+        k, c = UNITS[u]
+        nxt = UNITS[u + 1] + (all_b,) if u < last else (0, 0, rest)
+        if u < last:
+            wait_q(*UNITS[u + 1])
+        r = relays.get(u)
+        if r is not None:
+            relay_wait(r)
+        step(u % 2, (k, all_b, slot_of(k, c)), nxt, None if r is None else functools.partial(relay_merge, r))
+        send_unit(k, c)
+        if r is not None:
+            relay_send(r)
 
     def final(k, own):
         hh = (h if own else oh) * heads + k
         if own:
             parts = [(osend[own_slot(k, half), piece(h), :], lsend[own_slot(k, half), h]) for half in (0, 1)]
         else:
-            for rel in (0, 3):
-                arrived(ob.at[rel, hh], ors.at[rel, hh])
-                arrived(lb.at[rel, hh], lrs.at[rel, hh])
             parts = [(ob[rel, hh], lb[rel, hh]) for rel in (0, 3)]
         parts += [(ob[rel, hh], lb[rel, hh]) for rel in (LEFT, RIGHT)]
         ls = [p[1] for p in parts]
@@ -372,34 +372,48 @@
         o_out[:, hh] = acc.astype(BF).reshape(toks, grp, dim)
         lfin[pl.ds(hh, 1), :] = (m + jnp.log2(tot)) * float(math.log(2.0))
 
-    for k in range(heads):
+    def final_wait(k):
         for own in (True, False):
             hh = (h if own else oh) * heads + k
-            for rel in (LEFT, RIGHT):
+            for rel in (LEFT, RIGHT) if own else (0, LEFT, RIGHT, 3):
                 arrived(ob.at[rel, hh], ors.at[rel, hh])
                 arrived(lb.at[rel, hh], lrs.at[rel, hh])
-        for own in (True, False):
-            final(k, own)
-    l_out[...] = lfin[...]
-
-    def drain(k, carry):
-        cps = list(q_remote(k)) + [q_partner(k), forward(k, 0), forward(k, 1)]
-        for half in (0, 1):
-            cps += own_copies(k, half)
-        for c in (LEFT, RIGHT):
-            cps += side_copies(k, c)
-        for a in (0, 1):
-            cps += far_copies(k, a)
-            cps += merged_copies(k, a)
-        for cp in cps:
-            cp.wait_send()
-        return carry
-    lax.fori_loop(0, heads, drain, 0)
+
+    def final_both(k):
+        final(k, True)
+        final(k, False)
+
+    for k in range(heads):
+        extra = None
+        if k == 0:
+            relay_wait(heads - 1)
+            extra = functools.partial(relay_merge, heads - 1)
+        elif k >= 2:
+            final_wait(k - 2)
+            extra = functools.partial(final_both, k - 2)
+        step(k % 2, (k, rest, own_slot(k, 1)), (k + 1, 0, rest) if k + 1 < heads else None, extra)
+        start(own_copies(k, 1))
+        if k == 0:
+            relay_send(heads - 1)
+    for k in range(heads - 2, heads):
+        final_wait(k)
+    for k in range(heads - 2, heads):
+        final_both(k)
+
+    kh = 2 * heads
+    ltr[...] = jnp.concatenate([lfin[...], jnp.zeros((128 - kh, rows), F32)], axis=0).T
+    lse = None
+    for g in range(grp):
+        one = (lax.broadcasted_iota(jnp.int32, (128, kh * grp), 0) * grp + g == lax.broadcasted_iota(jnp.int32, (128, kh * grp), 1))
+        t = jnp.dot(ltr[pl.ds(g, toks, stride=grp), :], one.astype(F32), preferred_element_type=F32, precision=lax.Precision.HIGHEST)
+        lse = t if lse is None else lse + t
+    l_out[...] = lse
+
+    for buf, sem in ((qb.at[0:7 * heads // 2], qss), (osend.at[0:3 * heads], oss), (lsend.at[0:3 * heads], lss),
+                     (orel.at[0], rss), (lrel.at[0], rls), (kst.at[0:cl], kvs.at[0]), (vst.at[0:cl], kvs.at[1])):
+        arrived(buf, sem)
     for cp in new_remote():
         cp.wait_send()
-    for p in range(PARTS):
-        for cp in kv_remote(p):
-            cp.wait_send()
 
 
 def solution(mesh):
@@ -417,14 +431,14 @@
         q = queries.reshape(t, 2, hv, g, d)
         kc, vc = (a.reshape(cl, 2, hv, d) for a in (key_cache, value_cache))
         kn, vn = (a.reshape(t, 2, hv, d) for a in (key_new, value_new))
-        anyspec = pl.BlockSpec(memory_space=pl.ANY)
+        anyspec = pl.BlockSpec(memory_space=pltpu.HBM)
         vm = pl.BlockSpec(memory_space=pltpu.VMEM)
         dma = pltpu.SemaphoreType.DMA
         nres = 5 * hv
         o, l = pl.pallas_call(
             functools.partial(attend_kernel, n, d ** -0.5),
             name='attend',
-            out_shape=(jax.ShapeDtypeStruct((t, kh, g, d), BF), jax.ShapeDtypeStruct((kh, rows), F32)),
+            out_shape=(jax.ShapeDtypeStruct((t, kh, g, d), BF), jax.ShapeDtypeStruct((t, qh), F32)),
             in_specs=[pl.BlockSpec(memory_space=pltpu.SMEM)] + [anyspec] * 5,
             out_specs=(vm, vm),
             scratch_shapes=[
@@ -435,7 +449,7 @@
                 pltpu.VMEM((2 * t, hv, d), BF),
                 pltpu.VMEM((2 * t, hv, d), BF),
                 pltpu.VMEM((2, PREP * hv, d), F32),
-                pltpu.VMEM((4, hv, 2 * t, g, d), BF),
+                pltpu.VMEM((4 * hv, 2 * t, g, d), BF),
                 pltpu.VMEM((4, kh, rows, d), BF),
                 pltpu.VMEM((4, kh, 1, rows), F32),
                 pltpu.VMEM((nres, 2 * rows, d), BF),
@@ -446,16 +460,16 @@
                 pltpu.VMEM((nkeys, 2 * rows), F32),
                 pltpu.VMEM((2, 8, 2 * rows), F32),
                 pltpu.VMEM((kh, rows), F32),
-                dma((2, PARTS)), dma((2, PARTS)), dma((2, PARTS)),
+                pltpu.VMEM((rows, 128), F32),
+                dma((2, PARTS)), dma((2,)), dma((2, PARTS)),
                 dma((2,)), dma((2,)), dma((2,)),
-                dma((5, hv)), dma((4, 2, hv)), dma((2, hv)),
-                dma((nres, 2)), dma((4, kh)), dma((nres, 2)), dma((4, kh)),
-                dma((2, hv)), dma((2, hv)), dma((2, hv)), dma((2, hv)),
+                dma, dma((4, 2, hv)),
+                dma, dma((4, kh)), dma, dma((4, kh)),
+                dma, dma((2, hv)), dma, dma((2, hv)),
             ],
             compiler_params=pltpu.CompilerParams(collective_id=0, has_side_effects=True,
-                                                 vmem_limit_bytes=62 * 2 ** 20),
+                                                 vmem_limit_bytes=40 * 2 ** 20),
         )(prefix_len, q, kn, vn, kc, vc)
-        lse = l.reshape(kh, t, g).transpose(1, 0, 2).reshape(t, qh)
-        return o.reshape(t, qh, d), lse
+        return o.reshape(t, qh, d), l
 
     return jax.shard_map(local, mesh=mesh, in_specs=(tok, tok, tok, tok, tok, P('dp')), out_specs=(tok, tok), check_vma=False)

time: 49.3 us -> 50.4 us (1.022)
  local copies, waits for them, and re-layouts: 3.27 us -> 7.98 us
  Pallas kernels: 44.5 us -> 40.9 us
    unnamed x1 -> x12, local copies, waits for them, and re-layouts: 1.77 us -> 7.98 us
    pallas_call x1, Pallas kernels: 44.5 us -> 40.9 us  [local(): pl.pallas_call(functools.partial(attend_kernel, n, d ** (-0.5)), name='at...]
    pallas_call x1 -> x0, local copies, waits for them, and re-layouts: 0.8 us -> none  [local(): pl.pallas_call(functools.partial(attend_kernel, n, d ** (-0.5)), name='at...]
    transpose x1 -> x0, local copies, waits for them, and re-layouts: 0.7 us -> none  [local(): lse = l.reshape(kh, t, g).transpose(1, 0, 2).reshape(t, qh)]
where the time goes in v3:
time: 50.4 us; the launch traced here: 50.1 us
  Pallas kernels  40.9 us (81%)
  local copies, waits for them, and re-layouts  7.98 us (16%)
  between operations  1.3 us (3%)
    pallas_call x1, Pallas kernels, local(): pl.pallas_call(functools.partial(attend_kernel, n, d ** (-0.5)), name='at...  40.9 us
    unnamed x12, local copies, waits for them, and re-layouts  7.98 us

profile of v3, /device:TPU:113, one launch (start us, length us, event | category | flops | bytes accessed | tf_op | source)
XLA Modules:
  0.0 50.1 jit_solution(14576135360532754083)
XLA Ops:
  1.3 0.0 copy-start
  1.3 1.9 %copy-done = bf16[1536,8,128]{2,1,0:T(8,128)(2,1)S(1)} copy-done((bf16[1536,8,128]{2,1,0:T(8,128)(2,1)S(1)}, bf16[1536,8,128]{2,1,0:T(8,128)(2,1)}, u32[]{:S(2)}) %copy-start) | copy-done | bytes 3145752
  3.2 0.0 copy-start.1
  3.2 1.9 %copy-done.1 = bf16[1536,8,128]{2,1,0:T(8,128)(2,1)S(1)} copy-done((bf16[1536,8,128]{2,1,0:T(8,128)(2,1)S(1)}, bf16[1536,8,128]{2,1,0:T(8,128)(2,1)}, u32[]{:S(2)}) %copy-start.1) | copy-done | bytes 3145752
  5.1 0.0 copy-start.2
  5.1 1.0 %copy-done.2 = bf16[48,32,128]{2,1,0:T(8,128)(2,1)S(1)} copy-done((bf16[48,32,128]{2,1,0:T(8,128)(2,1)S(1)}, bf16[48,32,128]{2,1,0:T(8,128)(2,1)}, u32[]{:S(2)}) %copy-start.2) | copy-done | bytes 393240
  6.1 0.0 copy-start.3
  6.1 0.9 %copy-done.3 = bf16[48,8,128]{2,1,0:T(8,128)(2,1)S(1)} copy-done((bf16[48,8,128]{2,1,0:T(8,128)(2,1)S(1)}, bf16[48,8,128]{2,1,0:T(8,128)(2,1)}, u32[]{:S(2)}) %copy-start.3) | copy-done | bytes 98328
  6.9 0.0 copy-start.4
  7.0 0.9 %copy-done.4 = bf16[48,8,128]{2,1,0:T(8,128)(2,1)S(1)} copy-done((bf16[48,8,128]{2,1,0:T(8,128)(2,1)S(1)}, bf16[48,8,128]{2,1,0:T(8,128)(2,1)}, u32[]{:S(2)}) %copy-start.4) | copy-done | bytes 98328
  7.8 40.9 %attend.1 = (bf16[48,8,4,128]{3,2,1,0:T(4,128)(2,1)S(1)}, f32[48,32]{1,0:T(8,128)S(1)}) custom-call(s32[1]{0:T(128)S(6)} %copy.10.plen, bf16[48,2,4,4,128]{4,3,2,1,0:T(4,128)(2,1)S(1)} %bitcast.9, bf16[48,2,4,128]{3,2,1,0:T(4,128)(2,1)S(1)} %bitcast.10, bf16[48,2,4,128]{3,2,1,0:T(4,128)(2,1)S(1)} %bitcast.11, bf16[1536,2,4,128]{3,2,1,0:T(4,128)(2,1)S(1)} %bitcast.6, ...), custom_call_target="tpu_custom_call" | custom-call | tf_op jit(solution)/shard_map/attend/pallas_call | solution.py:438
  48.7 0.7 %copy.8 = f32[48,32]{0,1:T(8,128)} copy(f32[48,32]{1,0:T(8,128)S(1)} %get-tuple-element.7) | data formatting | bytes 12288
  49.4 0.7 %copy.11 = bf16[48,32,128]{2,1,0:T(8,128)(2,1)} copy(bf16[48,32,128]{2,1,0:T(8,128)(2,1)S(1)} %bitcast.8) | data formatting | bytes 786432
Async XLA Ops:
  1.3 1.9 %copy-start = (bf16[1536,8,128]{2,1,0:T(8,128)(2,1)S(1)}, bf16[1536,8,128]{2,1,0:T(8,128)(2,1)}, u32[]{:S(2)}) copy-start(bf16[1536,8,128]{2,1,0:T(8,128)(2,1)} %param.9) | copy-start | bytes 9437188
  3.2 1.9 %copy-start.1 = (bf16[1536,8,128]{2,1,0:T(8,128)(2,1)S(1)}, bf16[1536,8,128]{2,1,0:T(8,128)(2,1)}, u32[]{:S(2)}) copy-start(bf16[1536,8,128]{2,1,0:T(8,128)(2,1)} %param.10) | copy-start | bytes 9437188
  5.1 1.0 %copy-start.2 = (bf16[48,32,128]{2,1,0:T(8,128)(2,1)S(1)}, bf16[48,32,128]{2,1,0:T(8,128)(2,1)}, u32[]{:S(2)}) copy-start(bf16[48,32,128]{2,1,0:T(8,128)(2,1)} %param.6) | copy-start | bytes 1179652
  6.1 0.9 %copy-start.3 = (bf16[48,8,128]{2,1,0:T(8,128)(2,1)S(1)}, bf16[48,8,128]{2,1,0:T(8,128)(2,1)}, u32[]{:S(2)}) copy-start(bf16[48,8,128]{2,1,0:T(8,128)(2,1)} %param.7) | copy-start | bytes 294916
  6.9 0.9 %copy-start.4 = (bf16[48,8,128]{2,1,0:T(8,128)(2,1)S(1)}, bf16[48,8,128]{2,1,0:T(8,128)(2,1)}, u32[]{:S(2)}) copy-start(bf16[48,8,128]{2,1,0:T(8,128)(2,1)} %param.8) | copy-start | bytes 294916

commit v4 on v3

--- a/solution.py
+++ b/solution.py
@@ -469,7 +469,7 @@
             ],
             compiler_params=pltpu.CompilerParams(collective_id=0, has_side_effects=True,
                                                  vmem_limit_bytes=40 * 2 ** 20),
-        )(prefix_len, q, kn, vn, kc, vc)
+        )(prefix_len, *[pltpu.with_memory_space_constraint(a, pltpu.HBM) for a in (q, kn, vn, kc, vc)])
         return o.reshape(t, qh, d), l
 
     return jax.shard_map(local, mesh=mesh, in_specs=(tok, tok, tok, tok, tok, P('dp')), out_specs=(tok, tok), check_vma=False)

time: 50.4 us -> 43.8 us (0.87)
  local copies, waits for them, and re-layouts: 7.98 us -> 1.43 us
    unnamed x12 -> x2, local copies, waits for them, and re-layouts: 7.98 us -> 1.43 us
where the time goes in v4:
time: 43.8 us; the launch traced here: 43.7 us
  Pallas kernels  41 us (94%)
  local copies, waits for them, and re-layouts  1.43 us (3%)
  between operations  1.29 us (3%)
    pallas_call x1, Pallas kernels, local(): pl.pallas_call(functools.partial(attend_kernel, n, d ** (-0.5)), name='at...  41 us
    unnamed x2, local copies, waits for them, and re-layouts  1.43 us

profile of v4, /device:TPU:113, one launch (start us, length us, event | category | flops | bytes accessed | tf_op | source)
XLA Modules:
  0.0 43.7 jit_solution(13346722071092939804)
XLA Ops:
  1.3 41.0 %attend.1 = (bf16[48,8,4,128]{3,2,1,0:T(4,128)(2,1)S(1)}, f32[48,32]{1,0:T(8,128)S(1)}) custom-call(s32[1]{0:T(128)S(6)} %copy.10.plen, bf16[48,2,4,4,128]{4,3,2,1,0:T(4,128)(2,1)} %bitcast.9, bf16[48,2,4,128]{3,2,1,0:T(4,128)(2,1)} %bitcast.10, bf16[48,2,4,128]{3,2,1,0:T(4,128)(2,1)} %bitcast.11, bf16[1536,2,4,128]{3,2,1,0:T(4,128)(2,1)} %bitcast.7, ...), custom_call_target="tpu_custom_call" | custom-call | tf_op jit(solution)/shard_map/attend/pallas_call | solution.py:438
  42.3 0.7 %copy.8 = f32[48,32]{0,1:T(8,128)} copy(f32[48,32]{1,0:T(8,128)S(1)} %get-tuple-element.7) | data formatting | bytes 12288
  43.0 0.7 %copy.11 = bf16[48,32,128]{2,1,0:T(8,128)(2,1)} copy(bf16[48,32,128]{2,1,0:T(8,128)(2,1)S(1)} %bitcast.6) | data formatting | bytes 786432

commit v5 on v4

--- a/solution.py
+++ b/solution.py
@@ -13,23 +13,11 @@
 CH = 256
 PREP = 256
 PARTS = 3
-LOOPED = 8
 BF = jnp.bfloat16
 F32 = jnp.float32
 LEFT, RIGHT, FAR = 1, 2, 3
-UNITS = ((0, LEFT), (0, RIGHT), (1, LEFT), (1, RIGHT), (0, FAR), (1, FAR),
-         (2, LEFT), (2, RIGHT), (2, FAR), (3, FAR), (3, LEFT), (3, RIGHT))
-
-
-def pick(i, table):
-    out = table[0]
-    for j, v in enumerate(table[1:], 1):
-        out = jnp.where(i == j, v, out)
-    return out
-
-
 def attend_kernel(n, scale, plen, q, kn, vn, kc, vc, o_out, l_out,
-                  kb, vb, kst, vst, knst, vnst, prep, qb, ob, lb, osend, lsend, orel, lrel, s0, s1, mscr, lfin, ltr,
+                  kb, vb, kst, vst, knst, vnst, prep, qb, ob, lb, osend, lsend, orel, lrel, s0, s1, mscr, lfin, ltr, lim, oacc, lacc,
                   kvl, kvs, kvr, nvl, nvs, nvr, qss, qrs, oss, ors, lss, lrs, rss, rrs, rls, rlr):
     S = (s0, s1)
     toks, heads, grp, dim = q.shape[0], q.shape[2], q.shape[3], q.shape[4]
@@ -44,9 +32,6 @@
     xl, xr, xd = lax.rem(x + nch - 1, nch), lax.rem(x + 1, nch), lax.rem(x + 2, nch)
     chips = (x, xl, xr, xd)
 
-    def chip_of(c):
-        return chips[c] if isinstance(c, int) else pick(c, chips)
-
     def remote(src, dst, ss, rs, chip, core):
         return pltpu.make_async_remote_copy(src_ref=src, dst_ref=dst, send_sem=ss, recv_sem=rs,
                                             device_id={'cp': chip * 2 + core}, device_id_type=MESH)
@@ -106,6 +91,9 @@
         for way, rel in ((0, LEFT), (1, RIGHT)):
             q_arrived(rel, way, k)
             forward(k, way).start()
+        if k + heads // 2 < heads:
+            for cp in q_remote(k + heads // 2):
+                cp.start()
 
     for p in range(PARTS):
         for cp in kv_local(p):
@@ -119,28 +107,41 @@
         q_partner(k).start()
     for cp in new_remote():
         cp.start()
-    for k in range(heads):
+    for k in range(heads // 2):
         for cp in q_remote(k):
             cp.start()
     for p in range(PARTS):
         for cp in kv_remote(p):
             cp.start()
 
-    def split(kraw, vraw, count, base):
+    pref = plen[0] - x * (2 * cl)
+
+    def split(kraw, vraw, count, base, valid=None):
         prep[0, 0:count * heads] = kraw.reshape(count * heads, dim).astype(F32)
         prep[1, 0:count * heads] = vraw.reshape(count * heads, dim).astype(F32)
+
+        def rows_of(w, j):
+            v = prep[w, pl.ds(j, count, stride=heads), :]
+            if valid is not None:
+                v = jnp.where(lax.broadcasted_iota(jnp.int32, (count, 1), 0) < valid, v, 0.0)
+            return v.astype(BF)
+
         for j in range(heads):
-            kb[j, pl.ds(base, count), :] = prep[0, pl.ds(j, count, stride=heads), :].astype(BF)
-            vb[j, :, pl.ds(base, count)] = prep[1, pl.ds(j, count, stride=heads), :].astype(BF).T
-
-    def split_part(first):
-        def go(i, carry):
-            base = pl.multiple_of(first + i * PREP, PREP)
-            split(kst[pl.ds(base, PREP)], vst[pl.ds(base, PREP)], PREP, base)
-            return carry
-        lax.fori_loop(0, part // PREP, go, 0)
-
-    pref = plen[0] - x * (2 * cl)
+            kb[j, pl.ds(base, count), :] = rows_of(0, j)
+            vb[j, :, pl.ds(base, count)] = rows_of(1, j).T
+
+    def split_part(first, start_pos):
+        for may_hide in (False, True):
+            @pl.when(4 * (x + 1) > 3 * nch if may_hide else 4 * (x + 1) <= 3 * nch)
+            def _(may_hide=may_hide):
+                def go(i, carry):
+                    base = pl.multiple_of(first + i * PREP, PREP)
+                    valid = pref - (start_pos + i * PREP)
+                    split(kst[pl.ds(base, PREP)], vst[pl.ds(base, PREP)], PREP, base, valid if may_hide else None)
+                    lim[pl.ds(base, PREP), :] = jnp.where(lax.broadcasted_iota(jnp.int32, (PREP, 128), 0) < valid, float(jnp.finfo(F32).max), NEG)
+                    return carry
+                lax.fori_loop(0, part // PREP, go, 0)
+
     own_b = [(a, a + CH) for a in range(0, cl, CH)]
     oth_b = [(a, a + CH) for a in range(cl, 2 * cl, CH)]
     new_b = [(2 * cl, 2 * cl + 2 * toks)]
@@ -149,8 +150,7 @@
     def score_chunk(k, qv, chip, a, e, dst, mx):
         s = lax.dot_general(kb[k, a:e, :], qv, (((1,), (1,)), ((), ())), preferred_element_type=F32)
         if a < 2 * cl:
-            first = h * cl + a if a < cl else oh * cl + (a - cl)
-            s = jnp.where(lax.broadcasted_iota(jnp.int32, (e - a, 1), 0) < pref - first, s, NEG)
+            s = jnp.minimum(s, jnp.concatenate([lim[a:e, :]] * (cols // 128), axis=1))
         else:
             key = lax.broadcasted_iota(jnp.int32, (e - a, cols), 0)
             tok = lax.broadcasted_iota(jnp.int32, (e - a, cols), 1) // grp
@@ -162,34 +162,42 @@
     def value_chunk(k, a, e, src, mc, o, l):
         p = jnp.exp2(src[a:e, :] * c2 - mc)
         lsum = jnp.sum(p.reshape((e - a) // 8, 8, cols), axis=0)
-        oo = jnp.dot(vb[k, :, a:e], p.astype(BF), preferred_element_type=F32)
+        pp = p.astype(BF)
+        if cols % 256:
+            pp = jnp.concatenate([pp, pp[:, :256 - cols % 256]], axis=1)
+        oo = jnp.dot(vb[k, :, a:e], pp, preferred_element_type=F32)
         return (oo if o is None else o + oo), (lsum if l is None else l + lsum)
 
-    def step(slot, cur, nxt, extra=None):
+    def step(slot, cur, nxt, extras=()):
         mx = o = l = None
         if nxt is not None:
             k2, r2, b2 = nxt
             qv = qb[r2 * heads + k2].reshape(cols, dim)
-            chip = chip_of(r2)
         if cur is not None:
-            k, b1, u = cur
+            k, b1 = cur
             mc = mscr[slot][0:1, :]
         count = max(len(b2) if nxt is not None else 0, len(b1) if cur is not None else 0)
         for i in range(count):
-            if extra is not None and i == count // 3:
-                extra()
             if nxt is not None and i < len(b2):
-                mx = score_chunk(k2, qv, chip, *b2[i], S[1 - slot], mx)
+                mx = score_chunk(k2, qv, chips[r2], *b2[i], S[1 - slot], mx)
             if cur is not None and i < len(b1):
                 o, l = value_chunk(k, *b1[i], S[slot], mc, o, l)
+            for j, extra in enumerate(extras):
+                if i == min(1 + 2 * j, count - 1):
+                    extra()
         if nxt is not None:
             mscr[1 - slot] = jnp.broadcast_to(jnp.max(mx, axis=0, keepdims=True) * c2, (8, cols))
         if cur is not None:
             ls = jnp.sum(l, axis=0, keepdims=True)
-            osend[u] = (o * (1.0 / ls)).T.astype(BF)
-            lse = mc + jnp.log2(ls)
-            lsend[u, 0] = lse[:, :rows]
-            lsend[u, 1] = lse[:, rows:]
+            oacc[slot] = o[:, :cols]
+            lacc[slot, 0:1] = 1.0 / ls
+            lacc[slot, 1:2] = mc + jnp.log2(ls)
+
+    def close(u, slot):
+        osend[u] = (oacc[slot] * lacc[slot, 0:1]).T.astype(BF)
+        lse = lacc[slot, 1:2]
+        lsend[u, 0] = lse[:, :rows]
+        lsend[u, 1] = lse[:, rows:]
 
     def slot_of(k, c):
         return k * 3 + (c - 1)
@@ -213,10 +221,7 @@
 
     def side_copies(k, c):
         hh = hh_of(k)
-        if isinstance(c, int):
-            a, rel, chip = (c - 1), 3 - c, chips[c]
-        else:
-            a, rel, chip = c - 1, 3 - c, pick(c, chips)
+        a, rel, chip = (c - 1), 3 - c, chips[c]
         return result(slot_of(k, c), a, ob.at[rel, hh], lb.at[rel, hh], ors.at[rel, hh], lrs.at[rel, hh], chip, a)
 
     def far_copies(k, a):
@@ -261,96 +266,25 @@
             cp.start()
 
     def wait_q(k, c):
-        if isinstance(c, int):
-            if c != LEFT:
-                q_arrived(c, 0, k)
-            if c != RIGHT:
-                q_arrived(c, 1, k)
-        else:
-            @pl.when(c != LEFT)
-            def _():
-                q_arrived(c, 0, k)
-
-            @pl.when(c != RIGHT)
-            def _():
-                q_arrived(c, 1, k)
-
-    def send_unit(k, c):
-        if isinstance(c, int):
-            if c == FAR:
-                start(far_copies(k, 0))
-                start(far_copies(k, 1))
-            else:
-                start(side_copies(k, c))
-        else:
-            @pl.when(c == FAR)
-            def _():
-                start(far_copies(k, 0))
-                start(far_copies(k, 1))
-
-            @pl.when(c != FAR)
-            def _():
-                start(side_copies(k, c))
+        if c != LEFT:
+            q_arrived(c, 0, k)
+        if c != RIGHT:
+            q_arrived(c, 1, k)
 
     for p in range(PARTS):
         for cp in kv_local(p):
             cp.wait()
-        split_part(p * part)
-    wait_q(0, 0)
-    step(1, None, (0, 0, own_b))
-    for k in range(heads - 1):
-        wait_q(k + 1, 0)
-        step(k % 2, (k, own_b, own_slot(k, 0)), (k + 1, 0, own_b))
-        start(own_copies(k, 0))
-        if k == 1:
-            forwards(0)
-
-    for cp in new_local():
-        cp.wait()
-    for i, st in enumerate((knst, vnst)):
-        arrived(st.at[pl.ds(oh * toks, toks)], nvr.at[i])
-    split(knst[...], vnst[...], 2 * toks, 2 * cl)
-    for p in range(PARTS):
-        kv_arrived(p)
-        split_part(cl + p * part)
-    forwards(1)
-    wait_q(*UNITS[0])
-    step((heads - 1) % 2, (heads - 1, own_b, own_slot(heads - 1, 0)), UNITS[0] + (all_b,))
-    start(own_copies(heads - 1, 0))
-
-    def go(u, k, c, k2, c2_, slot):
-        wait_q(k2, c2_)
-        step(slot, (k, all_b, slot_of(k, c)), (k2, c2_, all_b))
-        send_unit(k, c)
-
-    hs, cs = [u[0] for u in UNITS], [u[1] for u in UNITS]
-
-    def pair(i, carry):
-        u = 2 * i
-        go(u, pick(u, hs), pick(u, cs), pick(u + 1, hs), pick(u + 1, cs), 0)
-
-        @pl.when(i < 2)
-        def _():
-            forwards(2 + i)
-        go(u + 1, pick(u + 1, hs), pick(u + 1, cs), pick(u + 2, hs), pick(u + 2, cs), 1)
-        return carry
-
-    lax.fori_loop(0, LOOPED // 2, pair, 0)
-    rest = oth_b + new_b
-    last = len(UNITS) - 1
-    relays = {LOOPED: 0, LOOPED + 1: 1, LOOPED + 2: 2}
-    for u in range(LOOPED, last + 1):
-        k, c = UNITS[u]
-        nxt = UNITS[u + 1] + (all_b,) if u < last else (0, 0, rest)
-        if u < last:
-            wait_q(*UNITS[u + 1])
-        r = relays.get(u)
-        if r is not None:
-            relay_wait(r)
-        step(u % 2, (k, all_b, slot_of(k, c)), nxt, None if r is None else functools.partial(relay_merge, r))
-        send_unit(k, c)
-        if r is not None:
-            relay_send(r)
+        split_part(p * part, h * cl + p * part)
+
+    def other_keys():
+        for cp in new_local():
+            cp.wait()
+        for i, st in enumerate((knst, vnst)):
+            arrived(st.at[pl.ds(oh * toks, toks)], nvr.at[i])
+        split(knst[...], vnst[...], 2 * toks, 2 * cl)
+        for p in range(PARTS):
+            kv_arrived(p)
+            split_part(cl + p * part, oh * cl + p * part)
 
     def final(k, own):
         hh = (h if own else oh) * heads + k
@@ -383,21 +317,61 @@
         final(k, True)
         final(k, False)
 
+    rest = oth_b + new_b
+    units = [(k, 0, own_b, own_slot(k, 0)) for k in range(heads)]
     for k in range(heads):
-        extra = None
-        if k == 0:
-            relay_wait(heads - 1)
-            extra = functools.partial(relay_merge, heads - 1)
-        elif k >= 2:
-            final_wait(k - 2)
-            extra = functools.partial(final_both, k - 2)
-        step(k % 2, (k, rest, own_slot(k, 1)), (k + 1, 0, rest) if k + 1 < heads else None, extra)
-        start(own_copies(k, 1))
-        if k == 0:
-            relay_send(heads - 1)
-    for k in range(heads - 2, heads):
+        units += [(k, c, all_b, slot_of(k, c)) for c in (FAR, LEFT, RIGHT)]
+    units += [(k, 0, rest, own_slot(k, 1)) for k in range(heads)]
+    nown, total = heads, len(units)
+    before = {1: [functools.partial(forwards, 0)], nown - 1: [other_keys, functools.partial(forwards, 1)]}
+    for k in range(2, heads):
+        before.setdefault(nown + 3 * (k - 2) + 1, []).append(functools.partial(forwards, k))
+    merge_at = {nown + 3 * k + 5: k for k in range(heads - 1)}
+    merge_at[total - heads + 1] = heads - 1
+
+    def send(i):
+        k, c, b, u = units[i]
+        if c == 0:
+            start(own_copies(k, 0 if i < nown else 1))
+        elif c == FAR:
+            start(far_copies(k, 0))
+            start(far_copies(k, 1))
+        else:
+            start(side_copies(k, c))
+
+    wait_q(0, 0)
+    step(1, None, (0, 0, own_b))
+    for i in range(total):
+        for f in before.get(i, ()):
+            f()
+        k, c, b, u = units[i]
+        nxt = None
+        if i + 1 < total:
+            k2, c2_, b2, _ = units[i + 1]
+            if not (c2_ == 0 and i + 1 >= nown):
+                wait_q(k2, c2_)
+            nxt = (k2, c2_, b2)
+        extras = []
+        if i > 0:
+            extras.append(functools.partial(close, units[i - 1][3], (i - 1) % 2))
+        r = merge_at.get(i)
+        if r is not None:
+            relay_wait(r)
+            extras.append(functools.partial(relay_merge, r))
+        if i == total - 1:
+            final_wait(0)
+            extras.append(functools.partial(final_both, 0))
+        step(i % 2, (k, b), nxt, extras)
+        if i > 0:
+            send(i - 1)
+        if r is not None:
+            relay_send(r)
+    final_wait(1)
+    close(units[-1][3], (total - 1) % 2)
+    final_both(1)
+    send(total - 1)
+    for k in range(2, heads):
         final_wait(k)
-    for k in range(heads - 2, heads):
         final_both(k)
 
     kh = 2 * heads
@@ -461,6 +435,9 @@
                 pltpu.VMEM((2, 8, 2 * rows), F32),
                 pltpu.VMEM((kh, rows), F32),
                 pltpu.VMEM((rows, 128), F32),
+                pltpu.VMEM((2 * cl, 128), F32),
+                pltpu.VMEM((2, d, 2 * rows), F32),
+                pltpu.VMEM((2, 8, 2 * rows), F32),
                 dma((2, PARTS)), dma((2,)), dma((2, PARTS)),
                 dma((2,)), dma((2,)), dma((2,)),
                 dma, dma((4, 2, hv)),

time: 43.8 us -> 42.3 us (0.966)
  Pallas kernels: 41 us -> 39.3 us
    pallas_call x1, Pallas kernels: 41 us -> 39.3 us  [local(): pl.pallas_call(functools.partial(attend_kernel, n, d ** (-0.5)), name='at...]
where the time goes in v5:
time: 42.3 us; the launch traced here: 42 us
  Pallas kernels  39.3 us (93%)
  local copies, waits for them, and re-layouts  1.43 us (3%)
  between operations  1.29 us (3%)
    pallas_call x1, Pallas kernels, local(): pl.pallas_call(functools.partial(attend_kernel, n, d ** (-0.5)), name='at...  39.3 us
    unnamed x2, local copies, waits for them, and re-layouts  1.43 us

profile of v5, /device:TPU:113, one launch (start us, length us, event | category | flops | bytes accessed | tf_op | source)
XLA Modules:
  0.0 42.0 jit_solution(1400699423376209400)
XLA Ops:
  1.3 39.3 %attend.1 = (bf16[48,8,4,128]{3,2,1,0:T(4,128)(2,1)S(1)}, f32[48,32]{1,0:T(8,128)S(1)}) custom-call(s32[1]{0:T(128)S(6)} %copy.10.plen, bf16[48,2,4,4,128]{4,3,2,1,0:T(4,128)(2,1)} %bitcast.9, bf16[48,2,4,128]{3,2,1,0:T(4,128)(2,1)} %bitcast.10, bf16[48,2,4,128]{3,2,1,0:T(4,128)(2,1)} %bitcast.11, bf16[1536,2,4,128]{3,2,1,0:T(4,128)(2,1)} %bitcast.7, ...), custom_call_target="tpu_custom_call" | custom-call | tf_op jit(solution)/shard_map/attend/pallas_call | solution.py:412
  40.6 0.7 %copy.8 = f32[48,32]{0,1:T(8,128)} copy(f32[48,32]{1,0:T(8,128)S(1)} %get-tuple-element.7) | data formatting | bytes 12288
  41.2 0.7 %copy.11 = bf16[48,32,128]{2,1,0:T(8,128)(2,1)} copy(bf16[48,32,128]{2,1,0:T(8,128)(2,1)S(1)} %bitcast.6) | data formatting | bytes 786432

commit v6 on v5

--- a/solution.py
+++ b/solution.py
@@ -16,6 +16,8 @@
 BF = jnp.bfloat16
 F32 = jnp.float32
 LEFT, RIGHT, FAR = 1, 2, 3
+ORDER = ((0, LEFT), (0, RIGHT), (0, FAR), (1, FAR), (1, LEFT), (1, RIGHT),
+         (2, FAR), (3, FAR), (2, LEFT), (2, RIGHT), (3, LEFT), (3, RIGHT))
 def attend_kernel(n, scale, plen, q, kn, vn, kc, vc, o_out, l_out,
                   kb, vb, kst, vst, knst, vnst, prep, qb, ob, lb, osend, lsend, orel, lrel, s0, s1, mscr, lfin, ltr, lim, oacc, lacc,
                   kvl, kvs, kvr, nvl, nvs, nvr, qss, qrs, oss, ors, lss, lrs, rss, rrs, rls, rlr):
@@ -319,15 +321,13 @@
 
     rest = oth_b + new_b
     units = [(k, 0, own_b, own_slot(k, 0)) for k in range(heads)]
-    for k in range(heads):
-        units += [(k, c, all_b, slot_of(k, c)) for c in (FAR, LEFT, RIGHT)]
+    units += [(k, c, all_b, slot_of(k, c)) for k, c in ORDER]
     units += [(k, 0, rest, own_slot(k, 1)) for k in range(heads)]
     nown, total = heads, len(units)
-    before = {1: [functools.partial(forwards, 0)], nown - 1: [other_keys, functools.partial(forwards, 1)]}
+    before = {2: [functools.partial(forwards, 0)], nown - 1: [other_keys, functools.partial(forwards, 1)]}
     for k in range(2, heads):
-        before.setdefault(nown + 3 * (k - 2) + 1, []).append(functools.partial(forwards, k))
-    merge_at = {nown + 3 * k + 5: k for k in range(heads - 1)}
-    merge_at[total - heads + 1] = heads - 1
+        before.setdefault(nown + k - 1, []).append(functools.partial(forwards, k))
+    merge_at = {10: 0, 12: 1, 15: 2, 17: 3}
 
     def send(i):
         k, c, b, u = units[i]
@@ -372,6 +372,7 @@
     send(total - 1)
     for k in range(2, heads):
         final_wait(k)
+    for k in range(2, heads):
         final_both(k)
 
     kh = 2 * heads

time: 42.3 us -> 42.9 us (1.014)
  Pallas kernels: 39.3 us -> 39.8 us
    pallas_call x1, Pallas kernels: 39.3 us -> 39.8 us  [local(): pl.pallas_call(functools.partial(attend_kernel, n, d ** (-0.5)), name='at...]
where the time goes in v6:
time: 42.9 us; the launch traced here: 42.5 us
  Pallas kernels  39.8 us (93%)
  local copies, waits for them, and re-layouts  1.43 us (3%)
  between operations  1.29 us (3%)
    pallas_call x1, Pallas kernels, local(): pl.pallas_call(functools.partial(attend_kernel, n, d ** (-0.5)), name='at...  39.8 us
    unnamed x2, local copies, waits for them, and re-layouts  1.43 us

profile of v6, /device:TPU:113, one launch (start us, length us, event | category | flops | bytes accessed | tf_op | source)
XLA Modules:
  0.0 42.5 jit_solution(6632983151097850865)
XLA Ops:
  1.3 39.8 %attend.1 = (bf16[48,8,4,128]{3,2,1,0:T(4,128)(2,1)S(1)}, f32[48,32]{1,0:T(8,128)S(1)}) custom-call(s32[1]{0:T(128)S(6)} %copy.10.plen, bf16[48,2,4,4,128]{4,3,2,1,0:T(4,128)(2,1)} %bitcast.9, bf16[48,2,4,128]{3,2,1,0:T(4,128)(2,1)} %bitcast.10, bf16[48,2,4,128]{3,2,1,0:T(4,128)(2,1)} %bitcast.11, bf16[1536,2,4,128]{3,2,1,0:T(4,128)(2,1)} %bitcast.7, ...), custom_call_target="tpu_custom_call" | custom-call | tf_op jit(solution)/shard_map/attend/pallas_call | solution.py:413
  41.0 0.7 %copy.8 = f32[48,32]{0,1:T(8,128)} copy(f32[48,32]{1,0:T(8,128)S(1)} %get-tuple-element.7) | data formatting | bytes 12288
  41.7 0.7 %copy.11 = bf16[48,32,128]{2,1,0:T(8,128)(2,1)} copy(bf16[48,32,128]{2,1,0:T(8,128)(2,1)S(1)} %bitcast.6) | data formatting | bytes 786432

commit v7 on v6

--- a/solution.py
+++ b/solution.py
@@ -93,8 +93,8 @@
         for way, rel in ((0, LEFT), (1, RIGHT)):
             q_arrived(rel, way, k)
             forward(k, way).start()
-        if k + heads // 2 < heads:
-            for cp in q_remote(k + heads // 2):
+        if k == 0:
+            for cp in q_remote(heads - 1):
                 cp.start()
 
     for p in range(PARTS):
@@ -109,7 +109,7 @@
         q_partner(k).start()
     for cp in new_remote():
         cp.start()
-    for k in range(heads // 2):
+    for k in range(heads - 1):
         for cp in q_remote(k):
             cp.start()
     for p in range(PARTS):
@@ -324,10 +324,10 @@
     units += [(k, c, all_b, slot_of(k, c)) for k, c in ORDER]
     units += [(k, 0, rest, own_slot(k, 1)) for k in range(heads)]
     nown, total = heads, len(units)
-    before = {2: [functools.partial(forwards, 0)], nown - 1: [other_keys, functools.partial(forwards, 1)]}
+    before = {nown - 1: [other_keys, functools.partial(forwards, 0), functools.partial(forwards, 1)]}
     for k in range(2, heads):
-        before.setdefault(nown + k - 1, []).append(functools.partial(forwards, k))
-    merge_at = {10: 0, 12: 1, 15: 2, 17: 3}
+        before.setdefault(nown + 2 * k - 3, []).append(functools.partial(forwards, k))
+    merge_at = {11: 0, 12: 1, 15: 2, 17: 3}
 
     def send(i):
         k, c, b, u = units[i]

time: 42.9 us -> 43.3 us (level)
  Pallas kernels: 39.8 us -> 40.5 us
    pallas_call x1, Pallas kernels: 39.8 us -> 40.5 us  [local(): pl.pallas_call(functools.partial(attend_kernel, n, d ** (-0.5)), name='at...]
where the time goes in v7:
time: 43.3 us
  Pallas kernels  40.5 us (94%)
  local copies, waits for them, and re-layouts  1.43 us (3%)
  between operations  1.29 us (3%)
    pallas_call x1, Pallas kernels, local(): pl.pallas_call(functools.partial(attend_kernel, n, d ** (-0.5)), name='at...  40.5 us
    unnamed x2, local copies, waits for them, and re-layouts  1.43 us

profile of v7, /device:TPU:113, one launch (start us, length us, event | category | flops | bytes accessed | tf_op | source)
XLA Modules:
  0.0 43.3 jit_solution(12320473105895217238)
XLA Ops:
  1.3 40.5 %attend.1 = (bf16[48,8,4,128]{3,2,1,0:T(4,128)(2,1)S(1)}, f32[48,32]{1,0:T(8,128)S(1)}) custom-call(s32[1]{0:T(128)S(6)} %copy.10.plen, bf16[48,2,4,4,128]{4,3,2,1,0:T(4,128)(2,1)} %bitcast.9, bf16[48,2,4,128]{3,2,1,0:T(4,128)(2,1)} %bitcast.10, bf16[48,2,4,128]{3,2,1,0:T(4,128)(2,1)} %bitcast.11, bf16[1536,2,4,128]{3,2,1,0:T(4,128)(2,1)} %bitcast.7, ...), custom_call_target="tpu_custom_call" | custom-call | tf_op jit(solution)/shard_map/attend/pallas_call | solution.py:413
  41.8 0.7 %copy.8 = f32[48,32]{0,1:T(8,128)} copy(f32[48,32]{1,0:T(8,128)S(1)} %get-tuple-element.7) | data formatting | bytes 12288
  42.5 0.7 %copy.11 = bf16[48,32,128]{2,1,0:T(8,128)(2,1)} copy(bf16[48,32,128]{2,1,0:T(8,128)(2,1)S(1)} %bitcast.6) | data formatting | bytes 786432

commit v8 on v6

--- a/solution.py
+++ b/solution.py
@@ -326,8 +326,8 @@
     nown, total = heads, len(units)
     before = {2: [functools.partial(forwards, 0)], nown - 1: [other_keys, functools.partial(forwards, 1)]}
     for k in range(2, heads):
-        before.setdefault(nown + k - 1, []).append(functools.partial(forwards, k))
-    merge_at = {10: 0, 12: 1, 15: 2, 17: 3}
+        before.setdefault(nown + 3 * k - 5, []).append(functools.partial(forwards, k))
+    merge_at = {11: 0, 13: 1, 15: 2, 17: 3}
 
     def send(i):
         k, c, b, u = units[i]

time: 42.9 us -> 42.6 us (level)
  no operation moved by 1% of the time
where the time goes in v8:
time: 42.6 us; the launch traced here: 42.5 us
  Pallas kernels  39.8 us (93%)
  local copies, waits for them, and re-layouts  1.43 us (3%)
  between operations  1.29 us (3%)
    pallas_call x1, Pallas kernels, local(): pl.pallas_call(functools.partial(attend_kernel, n, d ** (-0.5)), name='at...  39.8 us
    unnamed x2, local copies, waits for them, and re-layouts  1.43 us

profile of v8, /device:TPU:113, one launch (start us, length us, event | category | flops | bytes accessed | tf_op | source)
XLA Modules:
  0.0 42.5 jit_solution(10038782726408659404)
XLA Ops:
  1.3 39.8 %attend.1 = (bf16[48,8,4,128]{3,2,1,0:T(4,128)(2,1)S(1)}, f32[48,32]{1,0:T(8,128)S(1)}) custom-call(s32[1]{0:T(128)S(6)} %copy.10.plen, bf16[48,2,4,4,128]{4,3,2,1,0:T(4,128)(2,1)} %bitcast.9, bf16[48,2,4,128]{3,2,1,0:T(4,128)(2,1)} %bitcast.10, bf16[48,2,4,128]{3,2,1,0:T(4,128)(2,1)} %bitcast.11, bf16[1536,2,4,128]{3,2,1,0:T(4,128)(2,1)} %bitcast.7, ...), custom_call_target="tpu_custom_call" | custom-call | tf_op jit(solution)/shard_map/attend/pallas_call | solution.py:413
  41.1 0.7 %copy.8 = f32[48,32]{0,1:T(8,128)} copy(f32[48,32]{1,0:T(8,128)S(1)} %get-tuple-element.7) | data formatting | bytes 12288
  41.8 0.7 %copy.11 = bf16[48,32,128]{2,1,0:T(8,128)(2,1)} copy(bf16[48,32,128]{2,1,0:T(8,128)(2,1)S(1)} %bitcast.6) | data formatting | bytes 786432

commit v9 on v5

--- a/solution.py
+++ b/solution.py
@@ -16,6 +16,8 @@
 BF = jnp.bfloat16
 F32 = jnp.float32
 LEFT, RIGHT, FAR = 1, 2, 3
+ORDER = ((0, FAR), (0, LEFT), (0, RIGHT), (1, FAR), (1, LEFT), (1, RIGHT),
+         (2, FAR), (2, LEFT), (3, FAR), (2, RIGHT), (3, LEFT), (3, RIGHT))
 def attend_kernel(n, scale, plen, q, kn, vn, kc, vc, o_out, l_out,
                   kb, vb, kst, vst, knst, vnst, prep, qb, ob, lb, osend, lsend, orel, lrel, s0, s1, mscr, lfin, ltr, lim, oacc, lacc,
                   kvl, kvs, kvr, nvl, nvs, nvr, qss, qrs, oss, ors, lss, lrs, rss, rrs, rls, rlr):
@@ -319,8 +321,7 @@
 
     rest = oth_b + new_b
     units = [(k, 0, own_b, own_slot(k, 0)) for k in range(heads)]
-    for k in range(heads):
-        units += [(k, c, all_b, slot_of(k, c)) for c in (FAR, LEFT, RIGHT)]
+    units += [(k, c, all_b, slot_of(k, c)) for k, c in ORDER]
     units += [(k, 0, rest, own_slot(k, 1)) for k in range(heads)]
     nown, total = heads, len(units)
     before = {1: [functools.partial(forwards, 0)], nown - 1: [other_keys, functools.partial(forwards, 1)]}

time: 42.3 us -> 42.1 us (level); the launches traced: 42 us -> 41.3 us
  Pallas kernels: 39.3 us -> 38.6 us
    pallas_call x1, Pallas kernels: 39.3 us -> 38.6 us  [local(): pl.pallas_call(functools.partial(attend_kernel, n, d ** (-0.5)), name='at...]
where the time goes in v9:
time: 42.1 us; the launch traced here: 41.3 us
  Pallas kernels  38.6 us (92%)
  local copies, waits for them, and re-layouts  1.43 us (3%)
  between operations  1.29 us (3%)
    pallas_call x1, Pallas kernels, local(): pl.pallas_call(functools.partial(attend_kernel, n, d ** (-0.5)), name='at...  38.6 us
    unnamed x2, local copies, waits for them, and re-layouts  1.43 us

profile of v9, /device:TPU:113, one launch (start us, length us, event | category | flops | bytes accessed | tf_op | source)
XLA Modules:
  0.0 41.3 jit_solution(14606169208345418349)
XLA Ops:
  1.3 38.6 %attend.1 = (bf16[48,8,4,128]{3,2,1,0:T(4,128)(2,1)S(1)}, f32[48,32]{1,0:T(8,128)S(1)}) custom-call(s32[1]{0:T(128)S(6)} %copy.10.plen, bf16[48,2,4,4,128]{4,3,2,1,0:T(4,128)(2,1)} %bitcast.9, bf16[48,2,4,128]{3,2,1,0:T(4,128)(2,1)} %bitcast.10, bf16[48,2,4,128]{3,2,1,0:T(4,128)(2,1)} %bitcast.11, bf16[1536,2,4,128]{3,2,1,0:T(4,128)(2,1)} %bitcast.7, ...), custom_call_target="tpu_custom_call" | custom-call | tf_op jit(solution)/shard_map/attend/pallas_call | solution.py:413
  39.9 0.7 %copy.8 = f32[48,32]{0,1:T(8,128)} copy(f32[48,32]{1,0:T(8,128)S(1)} %get-tuple-element.7) | data formatting | bytes 12288
  40.6 0.7 %copy.11 = bf16[48,32,128]{2,1,0:T(8,128)(2,1)} copy(bf16[48,32,128]{2,1,0:T(8,128)(2,1)S(1)} %bitcast.6) | data formatting | bytes 786432
